TPU v7x, 256 devices: a whole 4x4x8 slice. The times are simulated.
256 devices in a mesh: row: 8 (over y, z_hi), col: 32 (over z_lo, x, core).
Axes of the slice: x: 4, y: 4, z: 8 (z_hi: 2, z_lo: 4; z = z_hi * 4 + z_lo), core: 2. Of those that a mesh axis runs over, the one named last changes fastest.
Arguments:
- g_greater: bfloat16 [256, 256, 2, 4096], P('row', 'col'), may hold values from -6 to 6
- g_lesser: bfloat16 [256, 256, 2, 4096], P('row', 'col'), may hold values from -6 to 6
- coupling: float32 [64, 64], replicated, may hold values from 0.5 to 1.5
- partner: int32 [64], replicated, may hold values from 0 to 63, each once
- memory_start: int32 [256], P('row'), may hold values from 0 to 255, as said below
Outputs:
- collision: bfloat16 [256, 4, 2, 4096], P(('row', 'col'))
Inputs may be any that keep to these rules, and one draw needn't show every extreme that they name: partner names every orbital once. memory_start[t] lies between 0 and t.
All inputs are finite; a program needn't handle non-finite values.
Results may differ from a plain program's by a relative error of at most 0.0049.
Values may be sent and summed in bfloat16 or wider, within the bound.
No kernel may reach another device: no remote copies, remote signals or barrier semaphores. Data moves between devices by JAX's collectives and lax.ppermute only.
A program may use at most 192 MiB of HBM per device.

v0:
```python
import math

import jax
import jax.numpy as jnp
from jax import lax
from jax.sharding import PartitionSpec as P

TW = 4


def complex_product(left_real, left_imag, right_real, right_imag):
    return (
        left_real * right_real - left_imag * right_imag,
        left_real * right_imag + left_imag * right_real,
    )


def per_device(g_greater, g_lesser, coupling, partner, memory_start):
    tile_rows, tile_cols, components, pair_count = g_greater.shape
    row_count = lax.axis_size("row")
    col_count = lax.axis_size("col")
    orbits = coupling.shape[0]
    blocks = tile_rows // col_count
    window = TW
    layout_shape = (blocks, col_count, row_count, blocks, components, pair_count)
    got_greater, got_lesser = (
        lax.all_to_all(
            lax.all_to_all(
                g_greater.reshape(layout_shape), "row", split_axis=2, concat_axis=2, tiled=True
            ),
            "col",
            split_axis=1,
            concat_axis=1,
            tiled=True,
        ),
        lax.all_to_all(
            lax.all_to_all(
                g_lesser.reshape(layout_shape), "row", split_axis=2, concat_axis=2, tiled=True
            ),
            "col",
            split_axis=1,
            concat_axis=1,
            tiled=True,
        ),
    )
    split_shape = (blocks, col_count, row_count, blocks, components, orbits, orbits)
    flip_greater = (
        got_greater.reshape(split_shape)
        .transpose(3, 1, 2, 0, 4, 6, 5)
        .reshape(tile_rows, tile_cols, components, pair_count)
    )
    flip_lesser = (
        got_lesser.reshape(split_shape)
        .transpose(3, 1, 2, 0, 4, 6, 5)
        .reshape(tile_rows, tile_cols, components, pair_count)
    )
    permuted = (partner[:, None] * orbits + partner[None, :]).reshape(pair_count)
    weight = coupling.reshape(pair_count)
    perm_greater = jnp.take(g_greater, permuted, axis=3)
    perm_lesser = jnp.take(g_lesser, permuted, axis=3)

    def energy(direct, partnered, mirrored):
        first_pair = complex_product(
            direct[:, :, 0].astype(jnp.float32),
            direct[:, :, 1].astype(jnp.float32),
            partnered[:, :, 0].astype(jnp.float32),
            partnered[:, :, 1].astype(jnp.float32),
        )
        triple = complex_product(
            first_pair[0],
            first_pair[1],
            mirrored[:, :, 0].astype(jnp.float32),
            mirrored[:, :, 1].astype(jnp.float32),
        )
        return (weight * triple[0], weight * triple[1])

    greater_sig = energy(g_greater, perm_greater, flip_lesser)
    lesser_sig = energy(g_lesser, perm_lesser, flip_greater)
    first_times = lax.axis_index("row") * tile_rows + jnp.arange(tile_rows, dtype=jnp.int32)
    second_times = jnp.arange(tile_cols, dtype=jnp.int32) * col_count + lax.axis_index("col")
    live_mask = (second_times[None, :] >= memory_start[:, None]) & (
        second_times[None, :] <= first_times[:, None]
    )
    live_mask = live_mask[:, :, None]
    ret_real = jnp.where(live_mask, greater_sig[0] - lesser_sig[0], 0.0).astype(jnp.bfloat16)
    ret_imag = jnp.where(live_mask, greater_sig[1] - lesser_sig[1], 0.0).astype(jnp.bfloat16)
    retarded = jnp.stack([ret_real, ret_imag], axis=2).reshape(
        tile_rows, tile_cols, 2, orbits, orbits
    )
    left_matrix = retarded.transpose(0, 3, 2, 1, 4).reshape(
        tile_rows, orbits, 2 * tile_cols * orbits
    )
    lesser_slab = flip_lesser[:window].reshape(window, tile_cols, 2, orbits, orbits)
    slab_real = (
        lesser_slab[:, :, 0].transpose(1, 3, 0, 2).reshape(tile_cols * orbits, window * orbits)
    )
    slab_imag = (
        lesser_slab[:, :, 1].transpose(1, 3, 0, 2).reshape(tile_cols * orbits, window * orbits)
    )
    upper_half = jnp.concatenate([slab_real, slab_imag], axis=1)
    lower_half = jnp.concatenate([-slab_imag, slab_real], axis=1)
    right_matrix = jnp.concatenate([upper_half, lower_half], axis=0)
    product = jnp.dot(
        left_matrix.reshape(lax.axis_size("col") * blocks * orbits, 2 * tile_cols * orbits),
        right_matrix,
        preferred_element_type=jnp.float32,
    )
    summed = lax.psum_scatter(
        product.reshape(lax.axis_size("col") * blocks, orbits * 2 * window * orbits),
        "col",
        scatter_dimension=0,
        tiled=True,
    )
    scaling = 1.0 / (4.0 * math.sqrt(orbits * tile_rows * row_count))
    summed = summed.reshape(blocks, orbits, 2, window, orbits) * scaling
    return (
        summed.transpose(0, 3, 2, 1, 4).reshape(blocks, window, 2, pair_count).astype(jnp.bfloat16)
    )


def solution(mesh):
    return jax.shard_map(
        per_device,
        mesh=mesh,
        in_specs=(P("row", "col", None, None), P("row", "col", None, None), P(), P(), P("row")),
        out_specs=P(("row", "col"), None, None, None),
        check_vma=False,
    )
```

profile of v0, /device:TPU:1, one launch (start us, length us, event | category | flops | bytes accessed | tf_op | source)
XLA Modules:
  0.0 1032.9 jit_solution(10722541682727246017)
XLA Ops:
  6.5 10.0 copy.71
  16.5 11.6 %all-to-all-start = ((bf16[1,32,8,1,2,4096]{5,4,1,3,0,2:T(2,128)(2,1)}), bf16[1,32,8,1,2,4096]{5,4,1,3,0,2:T(2,128)(2,1)}, u32[]{:S(2)}, u32[]{:S(2)}) async-start(bf16[1,32,8,1,2,4096]{5,4,1,3,0,2:T(2,128)(2,1)} %bitcast.63), calls=%async_computation | async-start | bytes 8388608 | tf_op jit(solution)/shard_map/all_to_all | solution.py:37
  28.1 9.9 copy.70
  38.1 54.2 %all-to-all-done = bf16[1,32,8,1,2,4096]{5,4,1,3,0,2:T(2,128)(2,1)} async-done(((bf16[1,32,8,1,2,4096]{5,4,1,3,0,2:T(2,128)(2,1)}), bf16[1,32,8,1,2,4096]{5,4,1,3,0,2:T(2,128)(2,1)}, u32[]{:S(2)}, u32[]{:S(2)}) %all-to-all-start) | async-done | bytes 4194336 | tf_op jit(solution)/shard_map/all_to_all | solution.py:37
  99.0 10.1 copy.44
  109.2 62.7 %all-to-all-done.2 = bf16[1,32,8,1,2,4096]{5,4,1,3,0,2:T(2,128)(2,1)} async-done(((bf16[1,32,8,1,2,4096]{5,4,1,3,0,2:T(2,128)(2,1)}), bf16[1,32,8,1,2,4096]{5,4,1,3,0,2:T(2,128)(2,1)}, u32[]{:S(2)}, u32[]{:S(2)}) %all-to-all-start.2) | async-done | bytes 4194336 | tf_op jit(solution)/shard_map/all_to_all | solution.py:28
  171.9 64.6 %all-to-all-start.1 = ((bf16[1,32,8,1,2,4096]{5,4,2,3,0,1:T(2,128)(2,1)}), bf16[1,32,8,1,2,4096]{5,4,2,3,0,1:T(2,128)(2,1)}, u32[]{:S(2)}, u32[]{:S(2)}) async-start(bf16[1,32,8,1,2,4096]{5,4,2,3,0,1:T(2,128)(2,1)} %copy.44), calls=%async_computation.1 | async-start | bytes 8388608 | tf_op jit(solution)/shard_map/all_to_all | solution.py:36
  236.5 10.1 copy.52
  246.6 83.0 %all-to-all-done.1 = bf16[1,32,8,1,2,4096]{5,4,2,3,0,1:T(2,128)(2,1)} async-done(((bf16[1,32,8,1,2,4096]{5,4,2,3,0,1:T(2,128)(2,1)}), bf16[1,32,8,1,2,4096]{5,4,2,3,0,1:T(2,128)(2,1)}, u32[]{:S(2)}, u32[]{:S(2)}) %all-to-all-start.1) | async-done | bytes 4194336 | tf_op jit(solution)/shard_map/all_to_all | solution.py:36
  329.5 6.7 all-to-all-start.3
  336.5 25.3 %copy.40 = bf16[32,8,2,4096]{0,1,3,2:T(8,128)(2,1)} copy(bf16[32,8,2,4096]{3,2,1,0:T(2,128)(2,1)} %param.7) | data formatting | bytes 8388608 | tf_op args[0]
  361.8 25.3 %copy.48 = bf16[32,8,2,4096]{0,1,3,2:T(8,128)(2,1)} copy(bf16[32,8,2,4096]{3,2,1,0:T(2,128)(2,1)} %param.8) | data formatting | bytes 8388608 | tf_op args[1]
  387.3 38.2 %gather_fusion = bf16[4096,32,8,2]{1,2,3,0:T(8,128)(2,1)} fusion(bf16[32,8,2,4096]{0,1,3,2:T(8,128)(2,1)} %copy.40, s32[4096]{0:T(1024)S(1)} %fusion.28), kind=kCustom, calls=%fused_computation.clone | custom fusion | bytes 8404992 | tf_op jit(solution)/shard_map/jit(_take)/gather | solution.py:59
  425.5 19.8 %copy.41 = bf16[4096,32,8,2]{0,2,3,1:T(8,128)(2,1)} copy(bf16[4096,32,8,2]{1,2,3,0:T(8,128)(2,1)} %gather_fusion) | data formatting | bytes 8388608 | tf_op jit(solution)/shard_map/jit(_take)/gather | solution.py:59
  445.3 38.2 %gather_fusion.1 = bf16[4096,32,8,2]{1,2,3,0:T(8,128)(2,1)} fusion(bf16[32,8,2,4096]{0,1,3,2:T(8,128)(2,1)} %copy.48, s32[4096]{0:T(1024)S(1)} %fusion.28), kind=kCustom, calls=%fused_computation.1.clone | custom fusion | bytes 8404992 | tf_op jit(solution)/shard_map/jit(_take)/gather | solution.py:60
  483.5 19.8 %copy.49 = bf16[4096,32,8,2]{0,2,3,1:T(8,128)(2,1)} copy(bf16[4096,32,8,2]{1,2,3,0:T(8,128)(2,1)} %gather_fusion.1) | data formatting | bytes 8388608 | tf_op jit(solution)/shard_map/jit(_take)/gather | solution.py:60
  503.5 15.5 %fusion.30 = (bf16[32,8,1,4096]{3,2,1,0:T(2,128)(2,1)}, bf16[32,8,1,4096]{3,2,1,0:T(2,128)(2,1)}) fusion(bf16[32,8,2,4096]{3,2,1,0:T(2,128)(2,1)} %param.7), kind=kLoop, calls=%fused_computation.64 | loop fusion | bytes 8388608 | tf_op jit(solution)/shard_map/slice | solution.py:64
  519.0 10.5 %fusion.31 = (bf16[32,8,1,4096]{3,2,1,0:T(2,128)(2,1)}, bf16[32,8,1,4096]{3,2,1,0:T(2,128)(2,1)}) fusion(bf16[32,8,2,4096]{3,2,1,0:T(2,128)(2,1)S(1)} %copy-done), kind=kLoop, calls=%fused_computation.65 | loop fusion | bytes 8388608 | tf_op jit(solution)/shard_map/slice | solution.py:64
  533.4 14.2 %reshape.144 = bf16[1,32,8,1,2,64,64]{6,5,4,2,1,3,0:T(8,128)(2,1)} reshape(bf16[1,32,8,1,2,4096]{5,4,2,3,0,1:T(2,128)(2,1)} %all-to-all-done.1) | data formatting | bytes 8388608 | tf_op jit(solution)/shard_map/reshape | solution.py:53
  547.6 12.5 %copy.45 = bf16[1,32,8,1,2,64,64]{5,2,6,1,4,0,3:T(8,128)(2,1)} copy(bf16[1,32,8,1,2,64,64]{6,5,4,2,1,3,0:T(8,128)(2,1)} %reshape.144) | data formatting | bytes 8388608 | tf_op jit(solution)/shard_map/reshape | solution.py:53
  560.1 9.4 copy.46
  569.5 12.1 %reshape.145 = bf16[32,8,2,4096]{3,1,2,0:T(8,128)(2,1)} reshape(bf16[1,32,8,1,2,64,64]{6,5,2,4,1,3,0:T(8,128)(2,1)} %copy.46) | data formatting | bytes 8388608 | tf_op jit(solution)/shard_map/reshape | solution.py:55
  581.5 14.2 %reshape.147 = bf16[1,32,8,1,2,64,64]{6,5,4,2,1,3,0:T(8,128)(2,1)} reshape(bf16[1,32,8,1,2,4096]{5,4,2,3,0,1:T(2,128)(2,1)} %all-to-all-done.3) | data formatting | bytes 8388608 | tf_op jit(solution)/shard_map/reshape | solution.py:48
  595.7 11.9 %copy.53 = bf16[1,32,8,1,2,64,64]{5,6,2,4,1,0,3:T(8,128)(2,1)} copy(bf16[1,32,8,1,2,64,64]{6,5,4,2,1,3,0:T(8,128)(2,1)} %reshape.147) | data formatting | bytes 8388608 | tf_op jit(solution)/shard_map/reshape | solution.py:48
  607.6 12.4 %reshape.148 = bf16[32,8,2,4096]{3,1,2,0:T(8,128)(2,1)} reshape(bf16[1,32,8,1,2,64,64]{6,5,2,4,1,3,0:T(8,128)(2,1)} %bitcast.61) | data formatting | bytes 8388608 | tf_op jit(solution)/shard_map/reshape | solution.py:50
  620.1 23.3 %fusion.6 = bf16[32,8,1,4096]{3,1,2,0:T(8,128)(2,1)} fusion(f32[4096]{0:T(1024)S(1)} %mul.138, pred[32,8]{1,0:T(8,128)(4,1)S(1)} %compare_and_fusion.1, bf16[32,8,2,4096]{3,1,2,0:T(8,128)(2,1)} %reshape.148, bf16[32,8,2,4096]{3,1,2,0:T(8,128)(2,1)} %reshape.145, bf16[32,8,2,4096]{3,1,2,0:T(8,128)(2,1)} %get-tuple-element.13, ...), kind=kLoop, calls=%fused_computation.25 | loop fusion | flops 36700160 | bytes 27279616 | tf_op jit(solution)/shard_map/convert_element_type | solution.py:85
  643.5 20.3 %fusion.11 = bf16[32,8,1,4096]{3,1,2,0:T(8,128)(2,1)S(1)} fusion(f32[4096]{0:T(1024)S(1)} %mul.138, pred[32,8]{1,0:T(8,128)(4,1)S(1)} %compare_and_fusion.1, bf16[32,8,2,4096]{3,1,2,0:T(8,128)(2,1)S(1)} %copy-done.4, bf16[32,8,2,4096]{3,1,2,0:T(8,128)(2,1)S(1)} %copy-done.3, bf16[32,8,2,4096]{3,1,2,0:T(8,128)(2,1)S(1)} %copy-done.2, ...), kind=kLoop, calls=%fused_computation.30 | loop fusion | flops 36700160 | bytes 27279616 | tf_op jit(solution)/shard_map/convert_element_type | solution.py:86
  666.0 6.9 stack.9
  678.6 8.7 maximum_bitcast_fusion
  687.3 23.2 %copy.54 = bf16[32,64,2,8,64]{4,3,2,1,0:T(8,128)(2,1)} copy(bf16[32,64,2,8,64]{4,1,3,0,2:T(8,128)(2,1)} %maximum_bitcast_fusion) | data formatting | bytes 8388608 | tf_op jit(solution)/shard_map/transpose | solution.py:90
  710.5 12.0 %reshape_reshape.3 = bf16[2048,1024]{1,0:T(8,128)(2,1)} reshape(bf16[32,64,2,8,64]{4,3,2,1,0:T(8,128)(2,1)} %copy.54) | data formatting | bytes 8388608 | tf_op jit(solution)/shard_map/reshape;reshape | solution.py:104
  736.1 286.4 %all-reduce.3.cloned.1.call-done = f32[32,32768]{1,0:T(8,128)} async-done(((f32[32,32768]{1,0:T(8,128)}), f32[32,32768]{1,0:T(8,128)}) %all-reduce.3.cloned.1.call-update) | async-done | bytes 4194320
  (51 shorter events, 36.0 us)
Async XLA Ops:
  16.5 75.8 %all-to-all-start = ((bf16[1,32,8,1,2,4096]{5,4,1,3,0,2:T(2,128)(2,1)}), bf16[1,32,8,1,2,4096]{5,4,1,3,0,2:T(2,128)(2,1)}, u32[]{:S(2)}, u32[]{:S(2)}) async-start(bf16[1,32,8,1,2,4096]{5,4,1,3,0,2:T(2,128)(2,1)} %bitcast.63), calls=%async_computation | async-start | bytes 8388608 | tf_op jit(solution)/shard_map/all_to_all | solution.py:37
  92.3 79.6 %all-to-all-start.2 = ((bf16[1,32,8,1,2,4096]{5,4,1,3,0,2:T(2,128)(2,1)}), bf16[1,32,8,1,2,4096]{5,4,1,3,0,2:T(2,128)(2,1)}, u32[]{:S(2)}, u32[]{:S(2)}) async-start(bf16[1,32,8,1,2,4096]{5,4,1,3,0,2:T(2,128)(2,1)} %bitcast.62), calls=%async_computation.2 | async-start | bytes 8388608 | tf_op jit(solution)/shard_map/all_to_all | solution.py:28
  171.9 157.6 %all-to-all-start.1 = ((bf16[1,32,8,1,2,4096]{5,4,2,3,0,1:T(2,128)(2,1)}), bf16[1,32,8,1,2,4096]{5,4,2,3,0,1:T(2,128)(2,1)}, u32[]{:S(2)}, u32[]{:S(2)}) async-start(bf16[1,32,8,1,2,4096]{5,4,2,3,0,1:T(2,128)(2,1)} %copy.44), calls=%async_computation.1 | async-start | bytes 8388608 | tf_op jit(solution)/shard_map/all_to_all | solution.py:36
  329.5 252.0 %all-to-all-start.3 = ((bf16[1,32,8,1,2,4096]{5,4,2,3,0,1:T(2,128)(2,1)}), bf16[1,32,8,1,2,4096]{5,4,2,3,0,1:T(2,128)(2,1)}, u32[]{:S(2)}, u32[]{:S(2)}) async-start(bf16[1,32,8,1,2,4096]{5,4,2,3,0,1:T(2,128)(2,1)} %copy.52), calls=%async_computation.3 | async-start | bytes 8388608 | tf_op jit(solution)/shard_map/all_to_all | solution.py:27
  336.3 686.2 %all-reduce.3.cloned.1.call-start = ((), (), s32[]{:S(2)}) async-start(), calls=%async_computation.4 | async-start | bytes 8388608
  361.8 25.3 %copy-start.9 = (s32[64]{0:T(128)S(1)}, s32[64]{0:T(128)}, u32[]{:S(2)}) copy-start(s32[64]{0:T(128)} %param.10) | copy-start | bytes 772
  483.5 19.8 %copy-start.8 = (f32[64,64]{1,0:T(8,128)S(1)}, f32[64,64]{1,0:T(8,128)}, u32[]{:S(2)}) copy-start(f32[64,64]{1,0:T(8,128)} %param.9) | copy-start | bytes 49156
  483.5 19.9 %copy-start.10 = (s32[32]{0:T(128)S(1)}, s32[32]{0:T(128)}, u32[]{:S(2)}) copy-start(s32[32]{0:T(128)} %param.11) | copy-start | bytes 388
  503.5 15.5 %copy-start = (bf16[32,8,2,4096]{3,2,1,0:T(2,128)(2,1)S(1)}, bf16[32,8,2,4096]{3,2,1,0:T(2,128)(2,1)}, u32[]{:S(2)}) copy-start(bf16[32,8,2,4096]{3,2,1,0:T(2,128)(2,1)} %param.8) | copy-start | bytes 12582916
  519.0 10.5 %copy-start.5 = (bf16[4096,32,8,2]{0,2,3,1:T(8,128)(2,1)S(1)}, bf16[4096,32,8,2]{0,2,3,1:T(8,128)(2,1)}, u32[]{:S(2)}) copy-start(bf16[4096,32,8,2]{0,2,3,1:T(8,128)(2,1)} %copy.41) | copy-start | bytes 12582916
  519.0 10.5 %copy-start.6 = (bf16[4096,32,8,2]{0,2,3,1:T(8,128)(2,1)S(1)}, bf16[4096,32,8,2]{0,2,3,1:T(8,128)(2,1)}, u32[]{:S(2)}) copy-start(bf16[4096,32,8,2]{0,2,3,1:T(8,128)(2,1)} %copy.49) | copy-start | bytes 12582916
  620.1 23.4 %copy-start.1 = (bf16[32,8,2,4096]{3,1,2,0:T(8,128)(2,1)S(1)}, bf16[32,8,2,4096]{3,1,2,0:T(8,128)(2,1)}, u32[]{:S(2)}) copy-start(bf16[32,8,2,4096]{3,1,2,0:T(8,128)(2,1)} %get-tuple-element.12) | copy-start | bytes 12582916
  620.1 23.4 %copy-start.2 = (bf16[32,8,2,4096]{3,1,2,0:T(8,128)(2,1)S(1)}, bf16[32,8,2,4096]{3,1,2,0:T(8,128)(2,1)}, u32[]{:S(2)}) copy-start(bf16[32,8,2,4096]{3,1,2,0:T(8,128)(2,1)} %get-tuple-element.13) | copy-start | bytes 12582916
  620.1 23.4 %copy-start.3 = (bf16[32,8,2,4096]{3,1,2,0:T(8,128)(2,1)S(1)}, bf16[32,8,2,4096]{3,1,2,0:T(8,128)(2,1)}, u32[]{:S(2)}) copy-start(bf16[32,8,2,4096]{3,1,2,0:T(8,128)(2,1)} %reshape.145) | copy-start | bytes 12582916
  620.1 23.4 %copy-start.4 = (bf16[32,8,2,4096]{3,1,2,0:T(8,128)(2,1)S(1)}, bf16[32,8,2,4096]{3,1,2,0:T(8,128)(2,1)}, u32[]{:S(2)}) copy-start(bf16[32,8,2,4096]{3,1,2,0:T(8,128)(2,1)} %reshape.148) | copy-start | bytes 12582916
  710.5 12.0 %copy-start.7 = (bf16[4,8,2,64,64]{4,1,3,0,2:T(8,128)(2,1)S(1)}, bf16[4,8,2,64,64]{4,1,3,0,2:T(8,128)(2,1)}, u32[]{:S(2)}) copy-start(bf16[4,8,2,64,64]{4,1,3,0,2:T(8,128)(2,1)} %slice_bitcast_fusion) | copy-start | bytes 1572868
  734.8 0.7 copy-start.11
Sparse Core Ops, SparseCore 0:
  735.0 287.4 all-reduce.2
where the time goes:
time: 1040 us; the launch traced here: 1030 us
  waiting for transfers between devices  486 us (47%)
  local copies, waits for them, and re-layouts  377 us (36%)
  starting transfers between devices  89.9 us (9%)
  other arithmetic  58.8 us (6%)
  between operations  14 us (1%)
    unnamed x2, waiting for transfers between devices  286 us
    all_to_all x1, waiting for transfers between devices, per_device(): lax.all_to_all(lax.all_to_all(g_lesser.reshape(layout_shape), 'row', spli...  83 us
    unnamed x29, local copies, waits for them, and re-layouts  71.7 us
    all_to_all x1, starting transfers between devices, per_device(): lax.all_to_all(lax.all_to_all(g_lesser.reshape(layout_shape), 'row', spli...  64.6 us
    all_to_all x1, waiting for transfers between devices, per_device(): lax.all_to_all(g_greater.reshape(layout_shape), 'row', split_axis=2, conc...  62.7 us
    gather x2, local copies, waits for them, and re-layouts, per_device(): perm_greater = jnp.take(g_greater, permuted, axis=3)  58 us
    gather x2, local copies, waits for them, and re-layouts, per_device(): perm_lesser = jnp.take(g_lesser, permuted, axis=3)  58 us
    all_to_all x1, waiting for transfers between devices, per_device(): lax.all_to_all(g_lesser.reshape(layout_shape), 'row', split_axis=2, conca...  54.2 us
  transfers between devices with their start and end apart: 5, of which 4 were waited for; matrix products, arithmetic and copies ran while one was open for 27% of the time, Pallas kernels for 0%

commit v1 on v0

v1 whole, which is shorter than its diff:
```python
import math

import jax
import jax.numpy as jnp
from jax import lax
from jax.experimental import pallas as pl
from jax.experimental.pallas import tpu as pltpu
from jax.sharding import PartitionSpec as P

TW = 4
ORB = 64
PAIRS = 32
LANES = 128
GROUP = 4


def tile_view(array):
    rows, cols, comps, pairs = array.shape
    split = array.reshape(rows, cols, comps, pairs // LANES, LANES)
    return split.transpose(0, 1, 3, 2, 4).reshape(rows * cols, comps * (pairs // LANES), LANES)


def direct_kernel(tiles_ref, swap_ref, move_ref, move_perm_ref, weight_ref, out_ref, flat, turned, turned_perm, stage, stage_perm):
    tiles = tiles_ref.shape[0]
    groups = tiles // GROUP
    flat[...] = tiles_ref[...].reshape(tiles * 2 * PAIRS, LANES).astype(jnp.float32)

    def one_group(index, carry):
        for comp in range(2):
            base = index * (GROUP * 2 * PAIRS) + comp
            block = flat[pl.ds(base, GROUP * PAIRS, stride=2), :]
            swapped = jnp.dot(
                block.astype(jnp.bfloat16), swap_ref[...], preferred_element_type=jnp.float32
            )
            turned[...] = block.T
            turned_perm[...] = swapped.T
            row = pl.multiple_of(index * (2 * PAIRS) + comp * PAIRS, PAIRS)
            for part in range(4):
                start = (part // 2) * ORB + part % 2
                cols = slice(part * LANES, (part + 1) * LANES)
                stage[pl.ds(row, PAIRS), cols] = turned[pl.ds(start, PAIRS, stride=2), :].astype(
                    jnp.bfloat16
                )
                stage_perm[pl.ds(row, PAIRS), cols] = turned_perm[
                    pl.ds(start, PAIRS, stride=2), :
                ].astype(jnp.bfloat16)
        return carry

    lax.fori_loop(0, groups, one_group, 0)
    weight = weight_ref[...]

    def one_product(index, carry):
        row = pl.multiple_of(index * (2 * PAIRS), 2 * PAIRS)
        plain = jnp.dot(
            stage[pl.ds(row, 2 * PAIRS), :], move_ref[...], preferred_element_type=jnp.float32
        )
        moved = jnp.dot(
            stage_perm[pl.ds(row, 2 * PAIRS), :],
            move_perm_ref[...],
            preferred_element_type=jnp.float32,
        )
        for item in range(GROUP):
            cols = slice(item * LANES, (item + 1) * LANES)
            a_real = plain[:PAIRS, cols]
            a_imag = plain[PAIRS:, cols]
            b_real = moved[:PAIRS, cols]
            b_imag = moved[PAIRS:, cols]
            out_ref[index * GROUP + item, 0] = weight * (a_real * b_real - a_imag * b_imag)
            out_ref[index * GROUP + item, 1] = weight * (a_real * b_imag + a_imag * b_real)
        return carry

    lax.fori_loop(0, groups, one_product, 0)


def direct_part(tiles, swap, move, move_perm, weight, block=32):
    count = tiles.shape[0]
    return pl.pallas_call(
        direct_kernel,
        grid=(count // block,),
        in_specs=[
            pl.BlockSpec((block, 2 * PAIRS, LANES), lambda n: (n, 0, 0)),
            pl.BlockSpec(swap.shape, lambda n: (0, 0)),
            pl.BlockSpec(move.shape, lambda n: (0, 0)),
            pl.BlockSpec(move_perm.shape, lambda n: (0, 0)),
            pl.BlockSpec(weight.shape, lambda n: (0, 0)),
        ],
        out_specs=pl.BlockSpec((block, 2, PAIRS, LANES), lambda n: (n, 0, 0, 0)),
        out_shape=jax.ShapeDtypeStruct((count, 2, PAIRS, LANES), jnp.float32),
        scratch_shapes=[
            pltpu.VMEM((block * 2 * PAIRS, LANES), jnp.float32),
            pltpu.VMEM((LANES, LANES), jnp.float32),
            pltpu.VMEM((LANES, LANES), jnp.float32),
            pltpu.VMEM((block // GROUP * 2 * PAIRS, GROUP * LANES), jnp.bfloat16),
            pltpu.VMEM((block // GROUP * 2 * PAIRS, GROUP * LANES), jnp.bfloat16),
        ],
        cost_estimate=pl.CostEstimate(
            flops=count * 64 * 512 * 512, bytes_accessed=count * 49152, transcendentals=0
        ),
        name="direct_part",
    )(tiles, swap, move, move_perm, weight)


def mirror_kernel(direct_ref, tiles_ref, out_ref, flat):
    tiles = tiles_ref.shape[0]
    flat[...] = tiles_ref[...].reshape(tiles * 2 * PAIRS, LANES).astype(jnp.float32)

    def one_tile(index, carry):
        m_real = flat[pl.ds(index * 2 * PAIRS, PAIRS, stride=2), :]
        m_imag = flat[pl.ds(index * 2 * PAIRS + 1, PAIRS, stride=2), :]
        d_real = direct_ref[index, 0]
        d_imag = direct_ref[index, 1]
        out_ref[index, 0] = d_real * m_real - d_imag * m_imag
        out_ref[index, 1] = d_real * m_imag + d_imag * m_real
        return carry

    lax.fori_loop(0, tiles, one_tile, 0, unroll=4)


def mirror_part(direct, tiles, block=32):
    count = tiles.shape[0]
    full = pl.BlockSpec((block, 2, PAIRS, LANES), lambda n: (n, 0, 0, 0))
    return pl.pallas_call(
        mirror_kernel,
        grid=(count // block,),
        in_specs=[full, pl.BlockSpec((block, 2 * PAIRS, LANES), lambda n: (n, 0, 0))],
        out_specs=full,
        out_shape=jax.ShapeDtypeStruct(direct.shape, jnp.float32),
        scratch_shapes=[pltpu.VMEM((block * 2 * PAIRS, LANES), jnp.float32)],
        cost_estimate=pl.CostEstimate(
            flops=count * 65536, bytes_accessed=count * 81920, transcendentals=0
        ),
        name="mirror_part",
    )(direct, tiles)


def integral_kernel(live_ref, first_ref, direct_ref, tiles_ref, slab_ref, out_ref, flat, right):
    tiles = tiles_ref.shape[0]
    steps = tiles // out_ref.shape[0]
    step = pl.program_id(0)
    flat[...] = tiles_ref[...].reshape(tiles * 2 * PAIRS, LANES).astype(jnp.float32)
    for moment in range(out_ref.shape[0]):
        cols = slice(moment * LANES, (moment + 1) * LANES)
        for item in range(steps):
            index = moment * steps + item
            live = live_ref[step * tiles + index] > 0
            m_real = flat[pl.ds(index * 2 * PAIRS, PAIRS, stride=2), :]
            m_imag = flat[pl.ds(index * 2 * PAIRS + 1, PAIRS, stride=2), :]
            d_real = direct_ref[index, 0]
            d_imag = direct_ref[index, 1]
            ret_real = first_ref[index, 0] - (d_real * m_real - d_imag * m_imag)
            ret_imag = first_ref[index, 1] - (d_real * m_imag + d_imag * m_real)
            row = item * 2 * PAIRS
            right[row : row + PAIRS, cols] = jnp.where(live, ret_real, 0.0).astype(jnp.bfloat16)
            right[row + PAIRS : row + 2 * PAIRS, cols] = jnp.where(live, ret_imag, 0.0).astype(
                jnp.bfloat16
            )
    product = jnp.dot(slab_ref[...], right[...], preferred_element_type=jnp.float32)
    quarter = product.shape[0] // 4
    lower = lax.broadcasted_iota(jnp.int32, (quarter, LANES), 1) < ORB
    for moment in range(out_ref.shape[0]):
        cols = slice(moment * LANES, (moment + 1) * LANES)
        even_real = product[:quarter, cols]
        even_imag = product[quarter : 2 * quarter, cols]
        odd_real = product[2 * quarter : 3 * quarter, cols]
        odd_imag = product[3 * quarter :, cols]
        kept = jnp.where(lower, even_real, odd_imag)
        crossed = jnp.where(lower, even_imag, odd_real)
        out_ref[moment] = (kept + pltpu.roll(crossed, ORB, 1)).astype(out_ref.dtype)


def integral_part(live, first, direct, tiles, slab, moments=2):
    count = tiles.shape[0]
    rows = live.shape[0] // 8
    block = count // rows * moments
    full = pl.BlockSpec((block, 2, PAIRS, LANES), lambda n: (n, 0, 0, 0))
    return pl.pallas_call(
        integral_kernel,
        grid=(rows // moments,),
        in_specs=[
            pl.BlockSpec(memory_space=pltpu.SMEM),
            full,
            full,
            pl.BlockSpec((block, 2 * PAIRS, LANES), lambda n: (n, 0, 0)),
            pl.BlockSpec(slab.shape, lambda n: (0, 0)),
        ],
        out_specs=pl.BlockSpec((moments, TW * ORB, LANES), lambda n: (n, 0, 0)),
        out_shape=jax.ShapeDtypeStruct((rows, TW * ORB, LANES), jnp.bfloat16),
        scratch_shapes=[
            pltpu.VMEM((block * 2 * PAIRS, LANES), jnp.float32),
            pltpu.VMEM((slab.shape[1], moments * LANES), jnp.bfloat16),
        ],
        cost_estimate=pl.CostEstimate(
            flops=rows * 2 * 1024 * 512 * 128, bytes_accessed=count * 81920, transcendentals=0
        ),
        name="integral_part",
    )(live, first, direct, tiles, slab)


def per_device(g_greater, g_lesser, coupling, partner, memory_start):
    tile_rows, tile_cols, components, pair_count = g_greater.shape
    row_count = lax.axis_size("row")
    col_count = lax.axis_size("col")
    orbits = coupling.shape[0]
    both = ("col", "row")
    tiles_greater = tile_view(g_greater)
    tiles_lesser = tile_view(g_lesser)
    flip_lesser = lax.all_to_all(tiles_lesser, both, 0, 0, tiled=True)
    flip_greater = lax.all_to_all(tiles_greater, both, 0, 0, tiled=True)

    orbit_ids = jnp.arange(orbits, dtype=jnp.int32)
    one_hot = (partner[:, None] == orbit_ids[None, :]).astype(jnp.bfloat16)
    swap = jnp.kron(jnp.eye(2, dtype=jnp.bfloat16), one_hot.T)
    source = jnp.arange(GROUP * LANES, dtype=jnp.int32)
    src_ib = source // (2 * LANES)
    src_jb = source // LANES % 2
    src_item = source % LANES // PAIRS
    src_orbit = source % PAIRS * 2 + src_ib
    dst_item = source // LANES
    dst_jb = source // ORB % 2
    dst_orbit = source % ORB
    same = (src_item[:, None] == dst_item[None, :]) & (src_jb[:, None] == dst_jb[None, :])
    move = (same & (src_orbit[:, None] == dst_orbit[None, :])).astype(jnp.bfloat16)
    wanted = jnp.tile(partner, 2 * GROUP)
    move_perm = (same & (src_orbit[:, None] == wanted[None, :])).astype(jnp.bfloat16)
    weight = coupling.T.reshape(PAIRS, LANES)

    direct_lesser = direct_part(tiles_lesser, swap, move, move_perm, weight)
    direct_greater = direct_part(tiles_greater, swap, move, move_perm, weight)
    first = mirror_part(direct_greater, flip_lesser)

    window = flip_lesser[: TW * tile_cols].reshape(TW, tile_cols, PAIRS, 2, 2, orbits)
    slab_real = window[:, :, :, 0]
    slab_imag = window[:, :, :, 1]
    to_real = jnp.stack([slab_real, -slab_imag], axis=0)
    to_imag = jnp.stack([slab_imag, slab_real], axis=0)
    slab = jnp.stack([to_real, to_imag], axis=0)
    slab = slab.transpose(5, 0, 2, 6, 3, 1, 4).reshape(
        2 * 2 * TW * orbits, tile_cols * 2 * PAIRS
    )
    first_times = lax.axis_index("row") * tile_rows + jnp.arange(tile_rows, dtype=jnp.int32)
    second_times = jnp.arange(tile_cols, dtype=jnp.int32) * col_count + lax.axis_index("col")
    live = (second_times[None, :] >= memory_start[:, None]) & (
        second_times[None, :] <= first_times[:, None]
    )
    live = live.astype(jnp.int32).reshape(tile_rows * tile_cols)
    partial = integral_part(live, first, direct_lesser, flip_greater, slab)
    shares = lax.all_to_all(partial, "col", 0, 0, tiled=True)
    scaling = 1.0 / (4.0 * math.sqrt(orbits * tile_rows * row_count))
    summed = shares.astype(jnp.float32).sum(axis=0) * scaling
    summed = summed.reshape(TW, orbits, 2, orbits).transpose(0, 2, 3, 1)
    return summed.reshape(1, TW, 2, pair_count).astype(jnp.bfloat16)


def solution(mesh):
    return jax.shard_map(
        per_device,
        mesh=mesh,
        in_specs=(P("row", "col", None, None), P("row", "col", None, None), P(), P(), P("row")),
        out_specs=P(("row", "col"), None, None, None),
        check_vma=False,
    )
```

time: 1040 us -> 307 us (0.30)
  waiting for transfers between devices: 486 us -> 0.01 us
  local copies, waits for them, and re-layouts: 377 us -> 9.72 us
  blocking collectives: 0 us -> 171 us
  Pallas kernels: 0 us -> 115 us
  starting transfers between devices: 89.9 us -> 8.31 us
  other arithmetic: 58.8 us -> 3.07 us
  between operations: 14 us -> 0.13 us
    unnamed x2 -> x0, waiting for transfers between devices: 286 us -> none
    all_to_all x4 -> x1, waiting for transfers between devices: 200 us -> 0.01 us  [per_device(): flip_greater = lax.all_to_all(tiles_greater, both, 0, 0, tiled=True)]
    all_to_all x0 -> x2, blocking collectives: none -> 171 us  [the longest x1 113 us: per_device(): flip_lesser = lax.all_to_all(tiles_lesser, both, 0, 0, tiled=True)]
    gather x4 -> x0, local copies, waits for them, and re-layouts: 116 us -> none  [the longest x2 58 us: per_device(): perm_greater = jnp.take(g_greater, permuted, axis=3)]
    pallas_call x0 -> x4, Pallas kernels: none -> 115 us  [the longest x2 86.5 us: direct_part(): pl.pallas_call(direct_kernel, grid=(count // block,), in_specs=[pl.BlockS...]
    all_to_all x4 -> x1, starting transfers between devices: 89.7 us -> 8.31 us  [per_device(): flip_greater = lax.all_to_all(tiles_greater, both, 0, 0, tiled=True)]
    reshape x10 -> x4, local copies, waits for them, and re-layouts: 85.1 us -> 3.92 us  [the longest x2 2.84 us: per_device(): slab.transpose(5, 0, 2, 6, 3, 1, 4)]
    unnamed x29 -> x6, local copies, waits for them, and re-layouts: 71.7 us -> 0.01 us
  transfers between devices with their start and end apart: 5 -> 1, of which waited for: 4 -> 0; matrix products, arithmetic and copies ran while one was open for 27% -> 4% of each run, Pallas kernels for 0% -> 32%
where the time goes in v1:
time: 307 us; the launch traced here: 306 us
  blocking collectives  171 us (56%)
  Pallas kernels  115 us (37%)
  local copies, waits for them, and re-layouts  9.72 us (3%)
  starting transfers between devices  8.31 us (3%)
    all_to_all x1, blocking collectives, per_device(): flip_lesser = lax.all_to_all(tiles_lesser, both, 0, 0, tiled=True)  113 us
    pallas_call x2, Pallas kernels, direct_part(): pl.pallas_call(direct_kernel, grid=(count // block,), in_specs=[pl.BlockS...  86.5 us
    all_to_all x1, blocking collectives, per_device(): shares = lax.all_to_all(partial, 'col', 0, 0, tiled=True)  57.6 us
    pallas_call x1, Pallas kernels, integral_part(): pl.pallas_call(integral_kernel, grid=(rows // moments,), in_specs=[pl.Blo...  17.9 us
    pallas_call x1, Pallas kernels, mirror_part(): pl.pallas_call(mirror_kernel, grid=(count // block,), in_specs=[full, pl....  10.3 us
    all_to_all x1, starting transfers between devices, per_device(): flip_greater = lax.all_to_all(tiles_greater, both, 0, 0, tiled=True)  8.31 us
  transfers between devices with their start and end apart: 1, of which 0 were waited for; matrix products, arithmetic and copies ran while one was open for 4% of the time, Pallas kernels for 32%

profile of v1, /device:TPU:1, one launch (start us, length us, event | category | flops | bytes accessed | tf_op | source)
XLA Modules:
  0.0 306.4 jit_solution(12194145832642717256)
XLA Ops:
  0.0 112.9 %all_to_all.15.tiles_ref = bf16[256,64,128]{2,1,0:T(8,128)(2,1)} all-to-all(bf16[256,64,128]{2,1,0:T(8,128)(2,1)} %bitcast.28), channel_id=1, replica_groups=mesh['row'=8,'col'=32] {'col','row'}, dimensions={0} | all-to-all | bytes 8388608 | tf_op jit(solution)/shard_map/all_to_all | solution.py:207
  112.9 8.3 %all-to-all-start.1 = ((bf16[256,64,128]{2,1,0:T(8,128)(2,1)}), bf16[256,64,128]{2,1,0:T(8,128)(2,1)}, u32[]{:S(2)}, u32[]{:S(2)}) async-start(bf16[256,64,128]{2,1,0:T(8,128)(2,1)} %bitcast.30), calls=%async_computation.1 | async-start | bytes 8388608 | tf_op jit(solution)/shard_map/all_to_all | solution.py:208
  121.3 0.0 copy-done.1
  121.3 0.1 eq.128
  121.4 0.1 broadcast_multiply_fusion
  121.5 0.7 mul.59.swap_ref
  122.2 0.1 copy.29
  122.3 0.7 reshape.220.weight_ref
  123.0 0.0 copy-done.2
  123.0 0.1 and_convert_fusion.2
  123.1 0.1 copy.27
  123.1 0.7 reshape.225.live_ref
  123.8 1.5 and_convert_fusion
  125.3 43.2 %direct_part.2.direct_ref = f32[256,2,32,128]{3,2,1,0:T(8,128)} custom-call(bf16[256,64,128]{2,1,0:T(8,128)(2,1)} %bitcast.31, bf16[128,128]{1,0:T(8,128)(2,1)} %mul.59.swap_ref, bf16[512,512]{1,0:T(8,128)(2,1)} %get-tuple-element.10.move_ref, bf16[512,512]{1,0:T(8,128)(2,1)} %get-tuple-element.9.move_perm_ref, f32[32,128]{1,0:T(8,128)} %reshape.220.weight_ref), custom_call_target="tpu_custom_call" | custom-call | flops 4294967296 | bytes 12582912 | tf_op jit(solution)/shard_map/direct_part/pallas_call | solution.py:77
  168.5 43.3 %direct_part.3.direct_ref = f32[256,2,32,128]{3,2,1,0:T(8,128)} custom-call(bf16[256,64,128]{2,1,0:T(8,128)(2,1)} %bitcast.29, bf16[128,128]{1,0:T(8,128)(2,1)} %mul.59.swap_ref, bf16[512,512]{1,0:T(8,128)(2,1)} %get-tuple-element.10.move_ref, bf16[512,512]{1,0:T(8,128)(2,1)} %get-tuple-element.9.move_perm_ref, f32[32,128]{1,0:T(8,128)} %reshape.220.weight_ref), custom_call_target="tpu_custom_call" | custom-call | flops 4294967296 | bytes 12582912 | tf_op jit(solution)/shard_map/direct_part/pallas_call | solution.py:77
  211.8 0.4 reshape.223
  212.2 1.1 fusion.23
  213.4 0.1 fusion.22
  213.5 0.2 copy_bitcast_fusion
  213.7 0.5 maximum_bitcast_fusion.1
  214.2 0.5 maximum_bitcast_fusion
  214.7 1.8 copy.33
  216.5 1.5 reshape.224
  218.0 1.4 copy.34.slab_ref
  219.3 10.3 %mirror_part.1.first_ref = f32[256,2,32,128]{3,2,1,0:T(8,128)} custom-call(f32[256,2,32,128]{3,2,1,0:T(8,128)} %direct_part.2.direct_ref, bf16[256,64,128]{2,1,0:T(8,128)(2,1)} %all_to_all.15.tiles_ref), custom_call_target="tpu_custom_call" | custom-call | flops 16777216 | bytes 20971520 | tf_op jit(solution)/shard_map/mirror_part/pallas_call | solution.py:122
  229.6 0.0 all-to-all-done.1.tiles_ref
  229.6 17.9 %integral_part.1 = bf16[32,256,128]{2,1,0:T(8,128)(2,1)} custom-call(s32[256]{0:T(256)} %reshape.225.live_ref, f32[256,2,32,128]{3,2,1,0:T(8,128)} %mirror_part.1.first_ref, f32[256,2,32,128]{3,2,1,0:T(8,128)} %direct_part.3.direct_ref, bf16[256,64,128]{2,1,0:T(8,128)(2,1)} %all-to-all-done.1.tiles_ref, bf16[1024,512]{1,0:T(8,128)(2,1)} %copy.34.slab_ref), custom_call_target="tpu_custom_call" | custom-call | flops 4294967296 | bytes 20971520 | tf_op jit(solution)/shard_map/integral_part/pallas_call | solution.py:176
  247.5 57.6 %all_to_all.16 = bf16[32,256,128]{2,1,0:T(8,128)(2,1)S(1)} all-to-all(bf16[32,256,128]{2,1,0:T(8,128)(2,1)} %integral_part.1), channel_id=1, replica_groups=mesh['row'=8,'col'=32] {'col'}, dimensions={0} | all-to-all | bytes 4194304 | tf_op jit(solution)/shard_map/all_to_all | solution.py:247
  305.1 0.3 convert_reduce_fusion
  305.4 0.1 convert_element_type.61
  305.5 0.1 copy.35
  305.6 0.8 convert_element_type.63
  (15 shorter events, 0.1 us)
Async XLA Ops:
  112.9 8.3 %copy-start.1 = (s32[64]{0:T(128)S(1)}, s32[64]{0:T(128)}, u32[]{:S(2)}) copy-start(s32[64]{0:T(128)} %param.8) | copy-start | bytes 772
  112.9 9.3 %copy-start = (f32[64,64]{1,0:T(8,128)S(1)}, f32[64,64]{1,0:T(8,128)}, u32[]{:S(2)}) copy-start(f32[64,64]{1,0:T(8,128)} %param.7) | copy-start | bytes 49156
  112.9 10.1 %copy-start.2 = (s32[32]{0:T(128)S(1)}, s32[32]{0:T(128)}, u32[]{:S(2)}) copy-start(s32[32]{0:T(128)} %param.9) | copy-start | bytes 388
  112.9 116.6 %all-to-all-start.1 = ((bf16[256,64,128]{2,1,0:T(8,128)(2,1)}), bf16[256,64,128]{2,1,0:T(8,128)(2,1)}, u32[]{:S(2)}, u32[]{:S(2)}) async-start(bf16[256,64,128]{2,1,0:T(8,128)(2,1)} %bitcast.30), calls=%async_computation.1 | async-start | bytes 8388608 | tf_op jit(solution)/shard_map/all_to_all | solution.py:208
  168.5 43.3 %slice-start = ((bf16[256,64,128]{2,1,0:T(8,128)(2,1)}), bf16[32,64,128]{2,1,0:T(8,128)(2,1)S(1)}, s32[]{:S(2)}) async-start(bf16[256,64,128]{2,1,0:T(8,128)(2,1)} %all_to_all.15.tiles_ref), calls=%async_computation.3 | async-start | bytes 1048576 | tf_op jit(solution)/shard_map/slice | solution.py:231

commit v2 on v1

--- a/solution.py
+++ b/solution.py
@@ -133,67 +133,78 @@
     )(direct, tiles)
 
 
-def integral_kernel(live_ref, first_ref, direct_ref, tiles_ref, slab_ref, out_ref, flat, right):
-    tiles = tiles_ref.shape[0]
-    steps = tiles // out_ref.shape[0]
+def integral_kernel(parity_ref, live_ref, first_ref, direct_ref, tiles_ref, slab_ref, out_ref, flat, *rights):
+    moments, steps = tiles_ref.shape[:2]
+    pair = moments // len(rights)
     step = pl.program_id(0)
-    flat[...] = tiles_ref[...].reshape(tiles * 2 * PAIRS, LANES).astype(jnp.float32)
-    for moment in range(out_ref.shape[0]):
-        cols = slice(moment * LANES, (moment + 1) * LANES)
-        for item in range(steps):
-            index = moment * steps + item
-            live = live_ref[step * tiles + index] > 0
-            m_real = flat[pl.ds(index * 2 * PAIRS, PAIRS, stride=2), :]
-            m_imag = flat[pl.ds(index * 2 * PAIRS + 1, PAIRS, stride=2), :]
-            d_real = direct_ref[index, 0]
-            d_imag = direct_ref[index, 1]
-            ret_real = first_ref[index, 0] - (d_real * m_real - d_imag * m_imag)
-            ret_imag = first_ref[index, 1] - (d_real * m_imag + d_imag * m_real)
-            row = item * 2 * PAIRS
-            right[row : row + PAIRS, cols] = jnp.where(live, ret_real, 0.0).astype(jnp.bfloat16)
-            right[row + PAIRS : row + 2 * PAIRS, cols] = jnp.where(live, ret_imag, 0.0).astype(
-                jnp.bfloat16
-            )
-    product = jnp.dot(slab_ref[...], right[...], preferred_element_type=jnp.float32)
-    quarter = product.shape[0] // 4
+    flat[...] = tiles_ref[...].reshape(moments * steps * 2 * PAIRS, LANES).astype(jnp.float32)
+    slab = slab_ref[...]
+    quarter = slab.shape[0] // 4
     lower = lax.broadcasted_iota(jnp.int32, (quarter, LANES), 1) < ORB
-    for moment in range(out_ref.shape[0]):
-        cols = slice(moment * LANES, (moment + 1) * LANES)
-        even_real = product[:quarter, cols]
-        even_imag = product[quarter : 2 * quarter, cols]
-        odd_real = product[2 * quarter : 3 * quarter, cols]
-        odd_imag = product[3 * quarter :, cols]
-        kept = jnp.where(lower, even_real, odd_imag)
-        crossed = jnp.where(lower, even_imag, odd_real)
-        out_ref[moment] = (kept + pltpu.roll(crossed, ORB, 1)).astype(out_ref.dtype)
-
-
-def integral_part(live, first, direct, tiles, slab, moments=2):
-    count = tiles.shape[0]
-    rows = live.shape[0] // 8
-    block = count // rows * moments
-    full = pl.BlockSpec((block, 2, PAIRS, LANES), lambda n: (n, 0, 0, 0))
+    for half, right in enumerate(rights):
+        for inner in range(pair):
+            moment = half * pair + inner
+            time = (step * moments + moment) * 2 + parity_ref[0]
+            cols = slice(inner * LANES, (inner + 1) * LANES)
+            for item in range(steps):
+                live = live_ref[time * steps + item] > 0
+                base = (moment * steps + item) * 2 * PAIRS
+                m_real = flat[pl.ds(base, PAIRS, stride=2), :]
+                m_imag = flat[pl.ds(base + 1, PAIRS, stride=2), :]
+                d_real = direct_ref[moment, item, 0]
+                d_imag = direct_ref[moment, item, 1]
+                ret_real = first_ref[moment, item, 0] - (d_real * m_real - d_imag * m_imag)
+                ret_imag = first_ref[moment, item, 1] - (d_real * m_imag + d_imag * m_real)
+                row = item * 2 * PAIRS
+                right[row : row + PAIRS, cols] = jnp.where(live, ret_real, 0.0).astype(
+                    jnp.bfloat16
+                )
+                right[row + PAIRS : row + 2 * PAIRS, cols] = jnp.where(
+                    live, ret_imag, 0.0
+                ).astype(jnp.bfloat16)
+        product = jnp.dot(slab, right[...], preferred_element_type=jnp.float32)
+        for inner in range(pair):
+            cols = slice(inner * LANES, (inner + 1) * LANES)
+            even_real = product[:quarter, cols]
+            even_imag = product[quarter : 2 * quarter, cols]
+            odd_real = product[2 * quarter : 3 * quarter, cols]
+            odd_imag = product[3 * quarter :, cols]
+            kept = jnp.where(lower, even_real, odd_imag)
+            crossed = jnp.where(lower, even_imag, odd_real)
+            out_ref[half * pair + inner] = kept + pltpu.roll(crossed, ORB, 1)
+
+
+def integral_part(parity, live, first, direct, tiles, slab, steps, moments=4, halves=2):
+    rows = tiles.shape[0] // steps
+    first = first.reshape(rows // 2, 2, steps, 2, PAIRS, LANES)
+    direct = direct.reshape(rows // 2, 2, steps, 2, PAIRS, LANES)
+    tiles = tiles.reshape(rows // 2, 2, steps, 2 * PAIRS, LANES)
+    full = pl.BlockSpec(
+        (moments, None, steps, 2, PAIRS, LANES), lambda n, p, v: (n, p[0], 0, 0, 0, 0)
+    )
     return pl.pallas_call(
         integral_kernel,
-        grid=(rows // moments,),
-        in_specs=[
-            pl.BlockSpec(memory_space=pltpu.SMEM),
-            full,
-            full,
-            pl.BlockSpec((block, 2 * PAIRS, LANES), lambda n: (n, 0, 0)),
-            pl.BlockSpec(slab.shape, lambda n: (0, 0)),
-        ],
-        out_specs=pl.BlockSpec((moments, TW * ORB, LANES), lambda n: (n, 0, 0)),
-        out_shape=jax.ShapeDtypeStruct((rows, TW * ORB, LANES), jnp.bfloat16),
-        scratch_shapes=[
-            pltpu.VMEM((block * 2 * PAIRS, LANES), jnp.float32),
-            pltpu.VMEM((slab.shape[1], moments * LANES), jnp.bfloat16),
-        ],
+        grid_spec=pltpu.PrefetchScalarGridSpec(
+            num_scalar_prefetch=2,
+            grid=(rows // 2 // moments,),
+            in_specs=[
+                full,
+                full,
+                pl.BlockSpec(
+                    (moments, None, steps, 2 * PAIRS, LANES), lambda n, p, v: (n, p[0], 0, 0, 0)
+                ),
+                pl.BlockSpec(slab.shape, lambda n, p, v: (0, 0)),
+            ],
+            out_specs=pl.BlockSpec((moments, TW * ORB, LANES), lambda n, p, v: (n, 0, 0)),
+            scratch_shapes=[pltpu.VMEM((moments * steps * 2 * PAIRS, LANES), jnp.float32)]
+            + [pltpu.VMEM((slab.shape[1], moments // halves * LANES), jnp.bfloat16)] * halves,
+        ),
+        out_shape=jax.ShapeDtypeStruct((rows // 2, TW * ORB, LANES), jnp.float32),
         cost_estimate=pl.CostEstimate(
-            flops=rows * 2 * 1024 * 512 * 128, bytes_accessed=count * 81920, transcendentals=0
+            flops=rows * 1024 * 512 * 128, bytes_accessed=rows * steps * 40960, transcendentals=0
         ),
         name="integral_part",
-    )(live, first, direct, tiles, slab)
+    )(parity, live, first, direct, tiles, slab)
 
 
 def per_device(g_greater, g_lesser, coupling, partner, memory_start):
@@ -205,7 +216,6 @@
     tiles_greater = tile_view(g_greater)
     tiles_lesser = tile_view(g_lesser)
     flip_lesser = lax.all_to_all(tiles_lesser, both, 0, 0, tiled=True)
-    flip_greater = lax.all_to_all(tiles_greater, both, 0, 0, tiled=True)
 
     orbit_ids = jnp.arange(orbits, dtype=jnp.int32)
     one_hot = (partner[:, None] == orbit_ids[None, :]).astype(jnp.bfloat16)
@@ -226,6 +236,10 @@
 
     direct_lesser = direct_part(tiles_lesser, swap, move, move_perm, weight)
     direct_greater = direct_part(tiles_greater, swap, move, move_perm, weight)
+    tiles_greater, direct_lesser, direct_greater = lax.optimization_barrier(
+        (tiles_greater, direct_lesser, direct_greater)
+    )
+    flip_greater = lax.all_to_all(tiles_greater, both, 0, 0, tiled=True)
     first = mirror_part(direct_greater, flip_lesser)
 
     window = flip_lesser[: TW * tile_cols].reshape(TW, tile_cols, PAIRS, 2, 2, orbits)
@@ -243,8 +257,18 @@
         second_times[None, :] <= first_times[:, None]
     )
     live = live.astype(jnp.int32).reshape(tile_rows * tile_cols)
-    partial = integral_part(live, first, direct_lesser, flip_greater, slab)
-    shares = lax.all_to_all(partial, "col", 0, 0, tiled=True)
+    core = lax.axis_index("col") % 2
+    away = integral_part(
+        jnp.reshape(1 - core, (1,)), live, first, direct_lesser, flip_greater, slab, tile_cols
+    )
+    arrived = lax.ppermute(away, "col", [(item, item ^ 1) for item in range(col_count)])
+    kept = integral_part(
+        jnp.reshape(core, (1,)), live, first, direct_lesser, flip_greater, slab, tile_cols
+    )
+    chips = [[2 * chip + side for chip in range(col_count // 2)] for side in range(2)]
+    shares = lax.all_to_all(
+        (kept + arrived).astype(jnp.bfloat16), "col", 0, 0, axis_index_groups=chips, tiled=True
+    )
     scaling = 1.0 / (4.0 * math.sqrt(orbits * tile_rows * row_count))
     summed = shares.astype(jnp.float32).sum(axis=0) * scaling
     summed = summed.reshape(TW, orbits, 2, orbits).transpose(0, 2, 3, 1)

time: 307 us -> 269 us (0.88)
  blocking collectives: 171 us -> 29 us
  waiting for transfers between devices: 0.01 us -> 83.2 us
  starting transfers between devices: 8.31 us -> 26.4 us
    all_to_all x2 -> x1, blocking collectives: 171 us -> 29 us  [per_device(): lax.all_to_all((kept + arrived).astype(jnp.bfloat16), 'col', 0, 0, axis_i...]
    all_to_all x1, waiting for transfers between devices: 0.01 us -> 76.6 us  [per_device(): flip_greater = lax.all_to_all(tiles_greater, both, 0, 0, tiled=True)]
    all_to_all x0 -> x1, starting transfers between devices: none -> 16.6 us  [per_device(): flip_lesser = lax.all_to_all(tiles_lesser, both, 0, 0, tiled=True)]
    all_to_all x0 -> x1, waiting for transfers between devices: none -> 6.6 us  [per_device(): flip_lesser = lax.all_to_all(tiles_lesser, both, 0, 0, tiled=True)]
    pallas_call x1 -> x2, Pallas kernels: 17.9 us -> 17.3 us  [integral_part(): pl.pallas_call(integral_kernel, grid_spec=pltpu.PrefetchScalarGridSpec(nu...]
  transfers between devices with their start and end apart: 1 -> 3, of which waited for: 0 -> 2; matrix products, arithmetic and copies ran while one was open for 4% -> 5% of each run, Pallas kernels for 32% -> 39%
where the time goes in v2:
time: 269 us; the launch traced here: 268 us
  Pallas kernels  114 us (42%)
  waiting for transfers between devices  83.2 us (31%)
  blocking collectives  29 us (11%)
  starting transfers between devices  26.4 us (10%)
  local copies, waits for them, and re-layouts  10.8 us (4%)
  other arithmetic  4.73 us (2%)
    pallas_call x2, Pallas kernels, direct_part(): pl.pallas_call(direct_kernel, grid=(count // block,), in_specs=[pl.BlockS...  86.4 us
    all_to_all x1, waiting for transfers between devices, per_device(): flip_greater = lax.all_to_all(tiles_greater, both, 0, 0, tiled=True)  76.6 us
    all_to_all x1, blocking collectives, per_device(): lax.all_to_all((kept + arrived).astype(jnp.bfloat16), 'col', 0, 0, axis_i...  29 us
    pallas_call x2, Pallas kernels, integral_part(): pl.pallas_call(integral_kernel, grid_spec=pltpu.PrefetchScalarGridSpec(nu...  17.3 us
    all_to_all x1, starting transfers between devices, per_device(): flip_lesser = lax.all_to_all(tiles_lesser, both, 0, 0, tiled=True)  16.6 us
    pallas_call x1, Pallas kernels, mirror_part(): pl.pallas_call(mirror_kernel, grid=(count // block,), in_specs=[full, pl....  10.3 us
    all_to_all x1, starting transfers between devices, per_device(): flip_greater = lax.all_to_all(tiles_greater, both, 0, 0, tiled=True)  8.27 us
    all_to_all x1, waiting for transfers between devices, per_device(): flip_lesser = lax.all_to_all(tiles_lesser, both, 0, 0, tiled=True)  6.6 us
  transfers between devices with their start and end apart: 3, of which 2 were waited for; matrix products, arithmetic and copies ran while one was open for 5% of the time, Pallas kernels for 39%

profile of v2, /device:TPU:1, one launch (start us, length us, event | category | flops | bytes accessed | tf_op | source)
XLA Modules:
  0.0 268.4 jit_solution(8855293437517843635)
XLA Ops:
  0.0 16.6 %all-to-all-start = ((bf16[256,64,128]{2,1,0:T(8,128)(2,1)}), bf16[256,64,128]{2,1,0:T(8,128)(2,1)}, u32[]{:S(2)}, u32[]{:S(2)}) async-start(bf16[256,64,128]{2,1,0:T(8,128)(2,1)} %bitcast.37), calls=%async_computation | async-start | bytes 8388608 | tf_op jit(solution)/shard_map/all_to_all | solution.py:218
  16.7 0.1 broadcast_multiply_fusion
  16.8 0.7 mul.59.swap_ref
  17.7 0.7 reshape.241.weight_ref
  18.4 1.5 and_convert_fusion
  19.9 43.2 %direct_part.2 = f32[256,2,32,128]{3,2,1,0:T(8,128)} custom-call(bf16[256,64,128]{2,1,0:T(8,128)(2,1)} %bitcast.38, bf16[128,128]{1,0:T(8,128)(2,1)} %mul.59.swap_ref, bf16[512,512]{1,0:T(8,128)(2,1)} %get-tuple-element.16.move_ref, bf16[512,512]{1,0:T(8,128)(2,1)} %get-tuple-element.15.move_perm_ref, f32[32,128]{1,0:T(8,128)} %reshape.241.weight_ref), custom_call_target="tpu_custom_call" | custom-call | flops 4294967296 | bytes 12582912 | tf_op jit(solution)/shard_map/direct_part/pallas_call | solution.py:77
  63.1 43.2 %direct_part.3.direct_ref = f32[256,2,32,128]{3,2,1,0:T(8,128)} custom-call(bf16[256,64,128]{2,1,0:T(8,128)(2,1)} %bitcast.39, bf16[128,128]{1,0:T(8,128)(2,1)} %mul.59.swap_ref, bf16[512,512]{1,0:T(8,128)(2,1)} %get-tuple-element.16.move_ref, bf16[512,512]{1,0:T(8,128)(2,1)} %get-tuple-element.15.move_perm_ref, f32[32,128]{1,0:T(8,128)} %reshape.241.weight_ref), custom_call_target="tpu_custom_call" | custom-call | flops 4294967296 | bytes 12582912 | tf_op jit(solution)/shard_map/direct_part/pallas_call | solution.py:77
  106.3 6.6 %all-to-all-done.tiles_ref = bf16[256,64,128]{2,1,0:T(8,128)(2,1)} async-done(((bf16[256,64,128]{2,1,0:T(8,128)(2,1)}), bf16[256,64,128]{2,1,0:T(8,128)(2,1)}, u32[]{:S(2)}, u32[]{:S(2)}) %all-to-all-start) | async-done | bytes 4194336 | tf_op jit(solution)/shard_map/all_to_all | solution.py:218
  112.9 8.3 %all-to-all-start.1 = ((bf16[256,64,128]{2,1,0:T(8,128)(2,1)}), bf16[256,64,128]{2,1,0:T(8,128)(2,1)}, u32[]{:S(2)}, u32[]{:S(2)}) async-start(bf16[256,64,128]{2,1,0:T(8,128)(2,1)} %bitcast.40), calls=%async_computation.1 | async-start | bytes 8388608 | tf_op jit(solution)/shard_map/all_to_all | solution.py:242
  121.3 0.1 copy.29
  121.4 0.7 reshape.248.live_ref
  122.1 1.1 slice.12
  123.1 0.4 reshape.245
  123.5 1.1 fusion.23
  124.7 0.1 fusion.22
  124.8 0.2 copy_bitcast_fusion
  125.1 0.5 maximum_bitcast_fusion.1
  125.5 0.5 maximum_bitcast_fusion
  126.0 1.8 copy.35
  127.8 1.5 reshape.246
  129.3 1.4 copy.36.slab_ref
  130.6 10.3 %mirror_part.1 = f32[256,2,32,128]{3,2,1,0:T(8,128)} custom-call(f32[256,2,32,128]{3,2,1,0:T(8,128)} %direct_part.3.direct_ref, bf16[256,64,128]{2,1,0:T(8,128)(2,1)} %all-to-all-done.tiles_ref), custom_call_target="tpu_custom_call" | custom-call | flops 16777216 | bytes 20971520 | tf_op jit(solution)/shard_map/mirror_part/pallas_call | solution.py:122
  140.9 76.6 %all-to-all-done.1 = bf16[256,64,128]{2,1,0:T(8,128)(2,1)} async-done(((bf16[256,64,128]{2,1,0:T(8,128)(2,1)}), bf16[256,64,128]{2,1,0:T(8,128)(2,1)}, u32[]{:S(2)}, u32[]{:S(2)}) %all-to-all-start.1) | async-done | bytes 4194336 | tf_op jit(solution)/shard_map/all_to_all | solution.py:242
  217.5 8.7 %integral_part.3 = f32[16,256,128]{2,1,0:T(8,128)} custom-call(s32[1]{0:T(128)} %bitcast.20.parity_ref, s32[256]{0:T(256)} %reshape.248.live_ref, f32[16,2,8,2,32,128]{5,4,3,2,1,0:T(8,128)} %bitcast.33, f32[16,2,8,2,32,128]{5,4,3,2,1,0:T(8,128)} %bitcast.35, bf16[16,2,8,64,128]{4,3,2,1,0:T(8,128)(2,1)} %bitcast.14.tiles_ref, bf16[1024,512]{1,0:T(8,128)(2,1)} %copy.36.slab_ref), custom_call_target="tpu_custom_call" | custom-call | flops 2147483648 | bytes 10485760 | tf_op jit(solution)/shard_map/integral_part/pallas_call | solution.py:185
  226.2 1.5 collective-permute-start
  227.7 8.7 %integral_part.2 = f32[16,256,128]{2,1,0:T(8,128)} custom-call(s32[1]{0:T(128)} %bitcast.parity_ref, s32[256]{0:T(256)} %reshape.248.live_ref, f32[16,2,8,2,32,128]{5,4,3,2,1,0:T(8,128)} %bitcast.34, f32[16,2,8,2,32,128]{5,4,3,2,1,0:T(8,128)} %bitcast.36, bf16[16,2,8,64,128]{4,3,2,1,0:T(8,128)(2,1)} %bitcast.14.tiles_ref, bf16[1024,512]{1,0:T(8,128)(2,1)} %copy.36.slab_ref), custom_call_target="tpu_custom_call" | custom-call | flops 2147483648 | bytes 10485760 | tf_op jit(solution)/shard_map/integral_part/pallas_call | solution.py:185
  236.4 1.8 add_convert_fusion
  238.2 29.0 %all_to_all.15 = bf16[16,256,128]{2,1,0:T(8,128)(2,1)S(1)} all-to-all(bf16[16,256,128]{2,1,0:T(8,128)(2,1)S(1)} %add_convert_fusion), channel_id=1, replica_groups={{0,2,4,6,8,10,12,14,16,18,20,22,24,26,28,30},{1,3,5,7,9,11,13,15,17,19,..., dimensions={0} | all-to-all | bytes 2097152 | tf_op jit(solution)/shard_map/all_to_all | solution.py:269
  267.2 0.1 convert_reduce_fusion
  267.3 0.1 convert_element_type.65
  267.4 0.1 copy.38
  267.6 0.8 convert_element_type.67
  (19 shorter events, 0.3 us)
Async XLA Ops:
  0.0 16.7 %copy-start.1 = (s32[64]{0:T(128)S(1)}, s32[64]{0:T(128)}, u32[]{:S(2)}) copy-start(s32[64]{0:T(128)} %param.8) | copy-start | bytes 772
  0.0 17.6 %copy-start = (f32[64,64]{1,0:T(8,128)S(1)}, f32[64,64]{1,0:T(8,128)}, u32[]{:S(2)}) copy-start(f32[64,64]{1,0:T(8,128)} %param.7) | copy-start | bytes 49156
  0.0 112.9 %all-to-all-start = ((bf16[256,64,128]{2,1,0:T(8,128)(2,1)}), bf16[256,64,128]{2,1,0:T(8,128)(2,1)}, u32[]{:S(2)}, u32[]{:S(2)}) async-start(bf16[256,64,128]{2,1,0:T(8,128)(2,1)} %bitcast.37), calls=%async_computation | async-start | bytes 8388608 | tf_op jit(solution)/shard_map/all_to_all | solution.py:218
  106.3 14.9 %copy-start.2 = (s32[32]{0:T(128)S(1)}, s32[32]{0:T(128)}, u32[]{:S(2)}) copy-start(s32[32]{0:T(128)} %param.9) | copy-start | bytes 388
  112.9 104.6 %all-to-all-start.1 = ((bf16[256,64,128]{2,1,0:T(8,128)(2,1)}), bf16[256,64,128]{2,1,0:T(8,128)(2,1)}, u32[]{:S(2)}, u32[]{:S(2)}) async-start(bf16[256,64,128]{2,1,0:T(8,128)(2,1)} %bitcast.40), calls=%async_computation.1 | async-start | bytes 8388608 | tf_op jit(solution)/shard_map/all_to_all | solution.py:242
  226.2 10.2 %collective-permute-start = (f32[16,256,128]{2,1,0:T(8,128)}, f32[16,256,128]{2,1,0:T(8,128)S(1)}, u32[]{:S(2)}, u32[]{:S(2)}) collective-permute-start(f32[16,256,128]{2,1,0:T(8,128)} %integral_part.3), channel_id=1, source_target_pairs={{0,1},{1,0},{2,3},{3,2},{4,5},{5,4},{6,7},{7,6},{8,9},{9,8},{10,11... | collective-permute-start | bytes 6291464 | tf_op jit(solution)/shard_map/ppermute | solution.py:264

commit v3 on v2

--- a/solution.py
+++ b/solution.py
@@ -12,6 +12,8 @@
 PAIRS = 32
 LANES = 128
 GROUP = 4
+CHIPS_Z = 4
+CHIPS_X = 4
 
 
 def tile_view(array):
@@ -133,78 +135,113 @@
     )(direct, tiles)
 
 
-def integral_kernel(parity_ref, live_ref, first_ref, direct_ref, tiles_ref, slab_ref, out_ref, flat, *rights):
-    moments, steps = tiles_ref.shape[:2]
-    pair = moments // len(rights)
+def integral_kernel(place_ref, live_ref, first_hbm, direct_hbm, tiles_hbm, slab_hbm, out_ref, first_buf, direct_buf, tiles_buf, slab_ref, flat, right, sems, slab_sem):
+    number, moments, steps = tiles_buf.shape[:3]
     step = pl.program_id(0)
-    flat[...] = tiles_ref[...].reshape(moments * steps * 2 * PAIRS, LANES).astype(jnp.float32)
-    slab = slab_ref[...]
-    quarter = slab.shape[0] // 4
-    lower = lax.broadcasted_iota(jnp.int32, (quarter, LANES), 1) < ORB
-    for half, right in enumerate(rights):
-        for inner in range(pair):
-            moment = half * pair + inner
-            time = (step * moments + moment) * 2 + parity_ref[0]
-            cols = slice(inner * LANES, (inner + 1) * LANES)
-            for item in range(steps):
-                live = live_ref[time * steps + item] > 0
-                base = (moment * steps + item) * 2 * PAIRS
-                m_real = flat[pl.ds(base, PAIRS, stride=2), :]
-                m_imag = flat[pl.ds(base + 1, PAIRS, stride=2), :]
-                d_real = direct_ref[moment, item, 0]
-                d_imag = direct_ref[moment, item, 1]
-                ret_real = first_ref[moment, item, 0] - (d_real * m_real - d_imag * m_imag)
-                ret_imag = first_ref[moment, item, 1] - (d_real * m_imag + d_imag * m_real)
-                row = item * 2 * PAIRS
-                right[row : row + PAIRS, cols] = jnp.where(live, ret_real, 0.0).astype(
+    slab_copy = pltpu.make_async_copy(slab_hbm, slab_ref, slab_sem)
+
+    def copies(index):
+        where = (place_ref[1] + index) % CHIPS_X
+        return [
+            pltpu.make_async_copy(
+                source.at[:, where, place_ref[0]], target.at[index], sems.at[kind, index]
+            )
+            for kind, (source, target) in enumerate(
+                ((tiles_hbm, tiles_buf), (first_hbm, first_buf), (direct_hbm, direct_buf))
+            )
+        ]
+
+    @pl.when(step == 0)
+    def _():
+        for index in range(number):
+            for copy in copies(index):
+                copy.start()
+            if index == 0:
+                slab_copy.start()
+
+    for copy in copies(step):
+        copy.wait()
+    first_ref = first_buf.at[step]
+    direct_ref = direct_buf.at[step]
+    across = (place_ref[1] + pl.program_id(0)) % CHIPS_X
+    depth = steps * 2 * PAIRS
+    flat[...] = tiles_buf[step].reshape(moments * depth, LANES).astype(jnp.float32)
+    low = lax.broadcasted_iota(jnp.int32, (PAIRS, LANES), 1) < ORB
+
+    def retarded(moment, item):
+        time = moment * (2 * CHIPS_X) + across * 2 + place_ref[0]
+        live = live_ref[time * steps + item] > 0
+        base = (moment * steps + item) * 2 * PAIRS
+        m_real = flat[pl.ds(base, PAIRS, stride=2), :]
+        m_imag = flat[pl.ds(base + 1, PAIRS, stride=2), :]
+        d_real = direct_ref[moment, item, 0]
+        d_imag = direct_ref[moment, item, 1]
+        ret_real = first_ref[moment, item, 0] - (d_real * m_real - d_imag * m_imag)
+        ret_imag = first_ref[moment, item, 1] - (d_real * m_imag + d_imag * m_real)
+        return jnp.where(live, ret_real, 0.0), jnp.where(live, ret_imag, 0.0)
+
+    for pair in range(moments // 2):
+        cols = slice(pair * LANES, (pair + 1) * LANES)
+        for item in range(steps):
+            left = retarded(2 * pair, item)
+            other = retarded(2 * pair + 1, item)
+            for comp in range(2):
+                row = (item * 2 + comp) * PAIRS
+                crossed = pltpu.roll(jnp.where(low, other[comp], left[comp]), ORB, 1)
+                right[row : row + PAIRS, cols] = jnp.where(low, left[comp], crossed).astype(
                     jnp.bfloat16
                 )
-                right[row + PAIRS : row + 2 * PAIRS, cols] = jnp.where(
-                    live, ret_imag, 0.0
+                right[depth + row : depth + row + PAIRS, cols] = jnp.where(
+                    low, crossed, other[comp]
                 ).astype(jnp.bfloat16)
-        product = jnp.dot(slab, right[...], preferred_element_type=jnp.float32)
-        for inner in range(pair):
-            cols = slice(inner * LANES, (inner + 1) * LANES)
-            even_real = product[:quarter, cols]
-            even_imag = product[quarter : 2 * quarter, cols]
-            odd_real = product[2 * quarter : 3 * quarter, cols]
-            odd_imag = product[3 * quarter :, cols]
-            kept = jnp.where(lower, even_real, odd_imag)
-            crossed = jnp.where(lower, even_imag, odd_real)
-            out_ref[half * pair + inner] = kept + pltpu.roll(crossed, ORB, 1)
-
-
-def integral_part(parity, live, first, direct, tiles, slab, steps, moments=4, halves=2):
-    rows = tiles.shape[0] // steps
-    first = first.reshape(rows // 2, 2, steps, 2, PAIRS, LANES)
-    direct = direct.reshape(rows // 2, 2, steps, 2, PAIRS, LANES)
-    tiles = tiles.reshape(rows // 2, 2, steps, 2 * PAIRS, LANES)
-    full = pl.BlockSpec(
-        (moments, None, steps, 2, PAIRS, LANES), lambda n, p, v: (n, p[0], 0, 0, 0, 0)
-    )
+
+    @pl.when(step == 0)
+    def _():
+        slab_copy.wait()
+
+    product = jnp.dot(slab_ref[...], right[...], preferred_element_type=jnp.float32)
+    half = product.shape[0] // 2
+    lower = lax.broadcasted_iota(jnp.int32, (half, LANES), 1) < ORB
+    for pair in range(moments // 2):
+        cols = slice(pair * LANES, (pair + 1) * LANES)
+        real = product[:half, cols]
+        imag = product[half:, cols]
+        crossed = pltpu.roll(jnp.where(lower, imag, real), ORB, 1)
+        slot = (2 * pair + CHIPS_Z - place_ref[2]) % CHIPS_Z
+        out_ref[slot] = jnp.where(lower, real, crossed)
+        out_ref[(slot + 1) % CHIPS_Z] = jnp.where(lower, crossed, imag)
+
+
+def integral_part(place, live, first, direct, tiles, slab, steps):
+    first = first.reshape(CHIPS_Z, CHIPS_X, 2, steps, 2, PAIRS, LANES)
+    direct = direct.reshape(CHIPS_Z, CHIPS_X, 2, steps, 2, PAIRS, LANES)
+    tiles = tiles.reshape(CHIPS_Z, CHIPS_X, 2, steps, 2 * PAIRS, LANES)
     return pl.pallas_call(
         integral_kernel,
         grid_spec=pltpu.PrefetchScalarGridSpec(
             num_scalar_prefetch=2,
-            grid=(rows // 2 // moments,),
-            in_specs=[
-                full,
-                full,
-                pl.BlockSpec(
-                    (moments, None, steps, 2 * PAIRS, LANES), lambda n, p, v: (n, p[0], 0, 0, 0)
-                ),
-                pl.BlockSpec(slab.shape, lambda n, p, v: (0, 0)),
+            grid=(CHIPS_X,),
+            in_specs=[pl.BlockSpec(memory_space=pl.ANY)] * 4,
+            out_specs=pl.BlockSpec(
+                (None, CHIPS_Z, TW * ORB, LANES), lambda n, p, v: (n, 0, 0, 0)
+            ),
+            scratch_shapes=[
+                pltpu.VMEM((CHIPS_X, CHIPS_Z, steps, 2, PAIRS, LANES), jnp.float32),
+                pltpu.VMEM((CHIPS_X, CHIPS_Z, steps, 2, PAIRS, LANES), jnp.float32),
+                pltpu.VMEM((CHIPS_X, CHIPS_Z, steps, 2 * PAIRS, LANES), jnp.bfloat16),
+                pltpu.VMEM(slab.shape, slab.dtype),
+                pltpu.VMEM((CHIPS_Z * steps * 2 * PAIRS, LANES), jnp.float32),
+                pltpu.VMEM((slab.shape[1], CHIPS_Z // 2 * LANES), jnp.bfloat16),
+                pltpu.SemaphoreType.DMA((3, CHIPS_X)),
+                pltpu.SemaphoreType.DMA,
             ],
-            out_specs=pl.BlockSpec((moments, TW * ORB, LANES), lambda n, p, v: (n, 0, 0)),
-            scratch_shapes=[pltpu.VMEM((moments * steps * 2 * PAIRS, LANES), jnp.float32)]
-            + [pltpu.VMEM((slab.shape[1], moments // halves * LANES), jnp.bfloat16)] * halves,
         ),
-        out_shape=jax.ShapeDtypeStruct((rows // 2, TW * ORB, LANES), jnp.float32),
+        out_shape=jax.ShapeDtypeStruct((CHIPS_X, CHIPS_Z, TW * ORB, LANES), jnp.float32),
         cost_estimate=pl.CostEstimate(
-            flops=rows * 1024 * 512 * 128, bytes_accessed=rows * steps * 40960, transcendentals=0
+            flops=16 * 1024 * 512 * 128, bytes_accessed=128 * 81920, transcendentals=0
         ),
         name="integral_part",
-    )(parity, live, first, direct, tiles, slab)
+    )(place, live, first, direct, tiles, slab)
 
 
 def per_device(g_greater, g_lesser, coupling, partner, memory_start):
@@ -248,8 +285,8 @@
     to_real = jnp.stack([slab_real, -slab_imag], axis=0)
     to_imag = jnp.stack([slab_imag, slab_real], axis=0)
     slab = jnp.stack([to_real, to_imag], axis=0)
-    slab = slab.transpose(5, 0, 2, 6, 3, 1, 4).reshape(
-        2 * 2 * TW * orbits, tile_cols * 2 * PAIRS
+    slab = slab.transpose(0, 2, 6, 5, 3, 1, 4).reshape(
+        2 * TW * orbits, 2 * tile_cols * 2 * PAIRS
     )
     first_times = lax.axis_index("row") * tile_rows + jnp.arange(tile_rows, dtype=jnp.int32)
     second_times = jnp.arange(tile_cols, dtype=jnp.int32) * col_count + lax.axis_index("col")
@@ -257,22 +294,50 @@
         second_times[None, :] <= first_times[:, None]
     )
     live = live.astype(jnp.int32).reshape(tile_rows * tile_cols)
-    core = lax.axis_index("col") % 2
+    column = lax.axis_index("col")
+    core = column % 2
+    along = column // 2 % CHIPS_X
+    depth = column // (2 * CHIPS_X)
     away = integral_part(
-        jnp.reshape(1 - core, (1,)), live, first, direct_lesser, flip_greater, slab, tile_cols
+        jnp.stack([1 - core, along, depth]), live, first, direct_lesser, flip_greater, slab, tile_cols
     )
     arrived = lax.ppermute(away, "col", [(item, item ^ 1) for item in range(col_count)])
     kept = integral_part(
-        jnp.reshape(core, (1,)), live, first, direct_lesser, flip_greater, slab, tile_cols
-    )
-    chips = [[2 * chip + side for chip in range(col_count // 2)] for side in range(2)]
-    shares = lax.all_to_all(
-        (kept + arrived).astype(jnp.bfloat16), "col", 0, 0, axis_index_groups=chips, tiled=True
-    )
+        jnp.stack([core, along, depth]), live, first, direct_lesser, flip_greater, slab, tile_cols
+    )
+    places = [
+        (z, x, side) for z in range(CHIPS_Z) for x in range(CHIPS_X) for side in range(2)
+    ]
+
+    def name_of(z, x, side):
+        return (z % CHIPS_Z * CHIPS_X + x % CHIPS_X) * 2 + side
+
+    summed = kept[0] + arrived[0]
+    parts = [
+        lax.ppermute(
+            (kept[shift] + arrived[shift]).astype(jnp.bfloat16),
+            "col",
+            [(name_of(z, x, side), name_of(z, x + shift, side)) for z, x, side in places],
+        )
+        for shift in range(1, CHIPS_X)
+    ]
+    for part in parts:
+        summed = summed + part.astype(jnp.float32)
+    total = summed[0]
+    parts = [
+        lax.ppermute(
+            summed[shift].astype(jnp.bfloat16),
+            "col",
+            [(name_of(z, x, side), name_of(z + shift, x, side)) for z, x, side in places],
+        )
+        for shift in range(1, CHIPS_Z)
+    ]
+    for part in parts:
+        total = total + part.astype(jnp.float32)
     scaling = 1.0 / (4.0 * math.sqrt(orbits * tile_rows * row_count))
-    summed = shares.astype(jnp.float32).sum(axis=0) * scaling
-    summed = summed.reshape(TW, orbits, 2, orbits).transpose(0, 2, 3, 1)
-    return summed.reshape(1, TW, 2, pair_count).astype(jnp.bfloat16)
+    total = total * scaling
+    total = total.reshape(TW, orbits, 2, orbits).transpose(0, 2, 3, 1)
+    return total.reshape(1, TW, 2, pair_count).astype(jnp.bfloat16)
 
 
 def solution(mesh):

time: 269 us -> 266 us (0.989)
  blocking collectives: 29 us -> 0 us
  waiting for transfers between devices: 83.2 us -> 96.8 us
  starting transfers between devices: 26.4 us -> 33.8 us
    all_to_all x1 -> x0, blocking collectives: 29 us -> none  [per_device(): lax.all_to_all((kept + arrived).astype(jnp.bfloat16), 'col', 0, 0, axis_i...]
    ppermute x0 -> x6, waiting for transfers between devices: none -> 13.9 us  [the longest x3 12.3 us: per_device(): lax.ppermute((kept[shift] + arrived[shift]).astype(jnp.bfloat16), 'col',...]
    ppermute x0 -> x6, starting transfers between devices: none -> 7.25 us  [the longest x3 4.27 us: per_device(): lax.ppermute(summed[shift].astype(jnp.bfloat16), 'col', [(name_of(z, x, s...]
  transfers between devices with their start and end apart: 3 -> 9, of which waited for: 2 -> 8; matrix products, arithmetic and copies ran while one was open for 5% -> 5% of each run, Pallas kernels for 39% -> 40%
where the time goes in v3:
time: 266 us; the launch traced here: 263 us
  Pallas kernels  115 us (43%)
  waiting for transfers between devices  96.8 us (36%)
  starting transfers between devices  33.8 us (13%)
  local copies, waits for them, and re-layouts  10.4 us (4%)
  other arithmetic  6.75 us (3%)
    pallas_call x2, Pallas kernels, direct_part(): pl.pallas_call(direct_kernel, grid=(count // block,), in_specs=[pl.BlockS...  86.5 us
    all_to_all x1, waiting for transfers between devices, per_device(): flip_greater = lax.all_to_all(tiles_greater, both, 0, 0, tiled=True)  76.4 us
    pallas_call x2, Pallas kernels, integral_part(): pl.pallas_call(integral_kernel, grid_spec=pltpu.PrefetchScalarGridSpec(nu...  18.2 us
    all_to_all x1, starting transfers between devices, per_device(): flip_lesser = lax.all_to_all(tiles_lesser, both, 0, 0, tiled=True)  16.6 us
    ppermute x3, waiting for transfers between devices, per_device(): lax.ppermute((kept[shift] + arrived[shift]).astype(jnp.bfloat16), 'col',...  12.3 us
    pallas_call x1, Pallas kernels, mirror_part(): pl.pallas_call(mirror_kernel, grid=(count // block,), in_specs=[full, pl....  10.3 us
    all_to_all x1, starting transfers between devices, per_device(): flip_greater = lax.all_to_all(tiles_greater, both, 0, 0, tiled=True)  8.27 us
    all_to_all x1, waiting for transfers between devices, per_device(): flip_lesser = lax.all_to_all(tiles_lesser, both, 0, 0, tiled=True)  6.55 us
  transfers between devices with their start and end apart: 9, of which 8 were waited for; matrix products, arithmetic and copies ran while one was open for 5% of the time, Pallas kernels for 40%

profile of v3, /device:TPU:1, one launch (start us, length us, event | category | flops | bytes accessed | tf_op | source)
XLA Modules:
  0.0 263.0 jit_solution(13262993516135498263)
XLA Ops:
  0.0 16.6 %all-to-all-start = ((bf16[256,64,128]{2,1,0:T(8,128)(2,1)}), bf16[256,64,128]{2,1,0:T(8,128)(2,1)}, u32[]{:S(2)}, u32[]{:S(2)}) async-start(bf16[256,64,128]{2,1,0:T(8,128)(2,1)} %bitcast.72), calls=%async_computation | async-start | bytes 8388608 | tf_op jit(solution)/shard_map/all_to_all | solution.py:255
  16.9 0.7 mul.57.swap_ref
  17.7 0.7 reshape.241.weight_ref
  18.4 1.5 and_convert_fusion
  19.9 43.3 %direct_part.2 = f32[256,2,32,128]{3,2,1,0:T(8,128)} custom-call(bf16[256,64,128]{2,1,0:T(8,128)(2,1)} %bitcast.73, bf16[128,128]{1,0:T(8,128)(2,1)} %mul.57.swap_ref, bf16[512,512]{1,0:T(8,128)(2,1)} %get-tuple-element.24.move_ref, bf16[512,512]{1,0:T(8,128)(2,1)} %get-tuple-element.23.move_perm_ref, f32[32,128]{1,0:T(8,128)} %reshape.241.weight_ref), custom_call_target="tpu_custom_call" | custom-call | flops 4294967296 | bytes 12582912 | tf_op jit(solution)/shard_map/direct_part/pallas_call | solution.py:79
  63.2 43.2 %direct_part.3.direct_ref = f32[256,2,32,128]{3,2,1,0:T(8,128)} custom-call(bf16[256,64,128]{2,1,0:T(8,128)(2,1)} %bitcast.74, bf16[128,128]{1,0:T(8,128)(2,1)} %mul.57.swap_ref, bf16[512,512]{1,0:T(8,128)(2,1)} %get-tuple-element.24.move_ref, bf16[512,512]{1,0:T(8,128)(2,1)} %get-tuple-element.23.move_perm_ref, f32[32,128]{1,0:T(8,128)} %reshape.241.weight_ref), custom_call_target="tpu_custom_call" | custom-call | flops 4294967296 | bytes 12582912 | tf_op jit(solution)/shard_map/direct_part/pallas_call | solution.py:79
  106.4 6.6 %all-to-all-done.tiles_ref = bf16[256,64,128]{2,1,0:T(8,128)(2,1)} async-done(((bf16[256,64,128]{2,1,0:T(8,128)(2,1)}), bf16[256,64,128]{2,1,0:T(8,128)(2,1)}, u32[]{:S(2)}, u32[]{:S(2)}) %all-to-all-start) | async-done | bytes 4194336 | tf_op jit(solution)/shard_map/all_to_all | solution.py:255
  112.9 8.3 %all-to-all-start.1 = ((bf16[256,64,128]{2,1,0:T(8,128)(2,1)}), bf16[256,64,128]{2,1,0:T(8,128)(2,1)}, u32[]{:S(2)}, u32[]{:S(2)}) async-start(bf16[256,64,128]{2,1,0:T(8,128)(2,1)} %bitcast.75), calls=%async_computation.1 | async-start | bytes 8388608 | tf_op jit(solution)/shard_map/all_to_all | solution.py:279
  121.4 0.7 reshape.247.live_ref
  122.1 0.6 add_add_fusion.1.place_ref
  122.7 1.1 slice.63
  124.1 1.1 fusion.40
  126.6 1.6 copy.27
  128.3 1.3 reshape.246
  129.5 1.3 copy.28.slab_hbm
  130.9 10.3 %mirror_part.1 = f32[256,2,32,128]{3,2,1,0:T(8,128)} custom-call(f32[256,2,32,128]{3,2,1,0:T(8,128)} %direct_part.3.direct_ref, bf16[256,64,128]{2,1,0:T(8,128)(2,1)} %all-to-all-done.tiles_ref), custom_call_target="tpu_custom_call" | custom-call | flops 16777216 | bytes 20971520 | tf_op jit(solution)/shard_map/mirror_part/pallas_call | solution.py:124
  141.2 76.4 %all-to-all-done.1 = bf16[256,64,128]{2,1,0:T(8,128)(2,1)} async-done(((bf16[256,64,128]{2,1,0:T(8,128)(2,1)}), bf16[256,64,128]{2,1,0:T(8,128)(2,1)}, u32[]{:S(2)}, u32[]{:S(2)}) %all-to-all-start.1) | async-done | bytes 4194336 | tf_op jit(solution)/shard_map/all_to_all | solution.py:279
  217.5 9.1 %integral_part.3 = f32[4,4,256,128]{3,2,1,0:T(8,128)} custom-call(s32[3]{0:T(128)} %add_add_fusion.1.place_ref, s32[256]{0:T(256)} %reshape.247.live_ref, f32[4,4,2,8,2,32,128]{6,5,4,3,2,1,0:T(8,128)} %bitcast.68, f32[4,4,2,8,2,32,128]{6,5,4,3,2,1,0:T(8,128)} %bitcast.70, bf16[4,4,2,8,64,128]{5,4,3,2,1,0:T(8,128)(2,1)} %bitcast.16.tiles_hbm, ...), custom_call_target="tpu_custom_call" | custom-call | flops 1073741824 | bytes 10485760 | tf_op jit(solution)/shard_map/integral_part/pallas_call | solution.py:219
  226.7 1.6 collective-permute-start
  228.3 0.6 add_add_fusion.place_ref
  228.9 9.1 %integral_part.2 = f32[4,4,256,128]{3,2,1,0:T(8,128)} custom-call(s32[3]{0:T(128)} %add_add_fusion.place_ref, s32[256]{0:T(256)} %reshape.247.live_ref, f32[4,4,2,8,2,32,128]{6,5,4,3,2,1,0:T(8,128)} %bitcast.69, f32[4,4,2,8,2,32,128]{6,5,4,3,2,1,0:T(8,128)} %bitcast.71, bf16[4,4,2,8,64,128]{5,4,3,2,1,0:T(8,128)(2,1)} %bitcast.16.tiles_hbm, ...), custom_call_target="tpu_custom_call" | custom-call | flops 1073741824 | bytes 10485760 | tf_op jit(solution)/shard_map/integral_part/pallas_call | solution.py:219
  238.0 1.5 fusion.7
  239.8 2.5 collective-permute-start.2
  242.6 7.0 %collective-permute-done.1 = bf16[4,256,128]{2,1,0:T(8,128)(2,1)S(1)} collective-permute-done((bf16[4,256,128]{2,1,0:T(8,128)(2,1)S(1)}, bf16[4,256,128]{2,1,0:T(8,128)(2,1)S(1)}, u32[]{:S(2)}, u32[]{:S(2)}) %collective-permute-start.1) | collective-permute-done | bytes 262176 | tf_op jit(solution)/shard_map/ppermute | solution.py:317
  249.5 4.3 %collective-permute-done.2 = bf16[4,256,128]{2,1,0:T(8,128)(2,1)S(1)} collective-permute-done((bf16[4,256,128]{2,1,0:T(8,128)(2,1)S(1)}, bf16[4,256,128]{2,1,0:T(8,128)(2,1)S(1)}, u32[]{:S(2)}, u32[]{:S(2)}) %collective-permute-start.2) | collective-permute-done | bytes 262176 | tf_op jit(solution)/shard_map/ppermute | solution.py:317
  253.9 1.0 collective-permute-done.3
  254.8 1.2 fusion.38
  256.5 2.3 collective-permute-start.5
  258.8 1.5 collective-permute-start.6
  260.3 0.8 collective-permute-done.4
  261.2 0.7 collective-permute-done.6
  262.2 0.8 convert_element_type.122
  (33 shorter events, 3.5 us)
Async XLA Ops:
  0.0 16.7 %copy-start.1 = (s32[64]{0:T(128)S(1)}, s32[64]{0:T(128)}, u32[]{:S(2)}) copy-start(s32[64]{0:T(128)} %param.8) | copy-start | bytes 772
  0.0 17.6 %copy-start = (f32[64,64]{1,0:T(8,128)S(1)}, f32[64,64]{1,0:T(8,128)}, u32[]{:S(2)}) copy-start(f32[64,64]{1,0:T(8,128)} %param.7) | copy-start | bytes 49156
  0.0 112.9 %all-to-all-start = ((bf16[256,64,128]{2,1,0:T(8,128)(2,1)}), bf16[256,64,128]{2,1,0:T(8,128)(2,1)}, u32[]{:S(2)}, u32[]{:S(2)}) async-start(bf16[256,64,128]{2,1,0:T(8,128)(2,1)} %bitcast.72), calls=%async_computation | async-start | bytes 8388608 | tf_op jit(solution)/shard_map/all_to_all | solution.py:255
  106.4 14.9 %copy-start.2 = (s32[32]{0:T(128)S(1)}, s32[32]{0:T(128)}, u32[]{:S(2)}) copy-start(s32[32]{0:T(128)} %param.9) | copy-start | bytes 388
  112.9 104.6 %all-to-all-start.1 = ((bf16[256,64,128]{2,1,0:T(8,128)(2,1)}), bf16[256,64,128]{2,1,0:T(8,128)(2,1)}, u32[]{:S(2)}, u32[]{:S(2)}) async-start(bf16[256,64,128]{2,1,0:T(8,128)(2,1)} %bitcast.75), calls=%async_computation.1 | async-start | bytes 8388608 | tf_op jit(solution)/shard_map/all_to_all | solution.py:279
  226.7 11.4 %collective-permute-start = (f32[4,4,256,128]{3,2,1,0:T(8,128)}, f32[4,4,256,128]{3,2,1,0:T(8,128)S(1)}, u32[]{:S(2)}, u32[]{:S(2)}) collective-permute-start(f32[4,4,256,128]{3,2,1,0:T(8,128)} %integral_part.3), channel_id=1, source_target_pairs={{0,1},{1,0},{2,3},{3,2},{4,5},{5,4},{6,7},{7,6},{8,9},{9,8},{10,11... | collective-permute-start | bytes 6291464 | tf_op jit(solution)/shard_map/ppermute | solution.py:304
  239.6 10.0 %collective-permute-start.1 = (bf16[4,256,128]{2,1,0:T(8,128)(2,1)S(1)}, bf16[4,256,128]{2,1,0:T(8,128)(2,1)S(1)}, u32[]{:S(2)}, u32[]{:S(2)}) collective-permute-start(bf16[4,256,128]{2,1,0:T(8,128)(2,1)S(1)} %get-tuple-element.13), channel_id=1, source_target_pairs={{0,2},{1,3},{2,4},{3,5},{4,6},{5,7},{6,0},{7,1},{8,10},{9,11},{10,... | collective-permute-start | bytes 786440 | tf_op jit(solution)/shard_map/ppermute | solution.py:317
  239.8 14.0 %collective-permute-start.2 = (bf16[4,256,128]{2,1,0:T(8,128)(2,1)S(1)}, bf16[4,256,128]{2,1,0:T(8,128)(2,1)S(1)}, u32[]{:S(2)}, u32[]{:S(2)}) collective-permute-start(bf16[4,256,128]{2,1,0:T(8,128)(2,1)S(1)} %get-tuple-element.15), channel_id=1, source_target_pairs={{0,4},{1,5},{2,6},{3,7},{4,0},{5,1},{6,2},{7,3},{8,12},{9,13},{10,... | collective-permute-start | bytes 786440 | tf_op jit(solution)/shard_map/ppermute | solution.py:317
  242.3 12.5 %collective-permute-start.3 = (bf16[4,256,128]{2,1,0:T(8,128)(2,1)S(1)}, bf16[4,256,128]{2,1,0:T(8,128)(2,1)S(1)}, u32[]{:S(2)}, u32[]{:S(2)}) collective-permute-start(bf16[4,256,128]{2,1,0:T(8,128)(2,1)S(1)} %get-tuple-element.14), channel_id=1, source_target_pairs={{0,6},{1,7},{2,0},{3,1},{4,2},{5,3},{6,4},{7,5},{8,14},{9,15},{10,... | collective-permute-start | bytes 786440 | tf_op jit(solution)/shard_map/ppermute | solution.py:317
  256.1 5.1 %collective-permute-start.4 = (bf16[256,128]{1,0:T(8,128)(2,1)S(1)}, bf16[256,128]{1,0:T(8,128)(2,1)S(1)}, u32[]{:S(2)}, u32[]{:S(2)}) collective-permute-start(bf16[256,128]{1,0:T(8,128)(2,1)S(1)} %get-tuple-element.20), channel_id=1, source_target_pairs={{0,8},{1,9},{2,10},{3,11},{4,12},{5,13},{6,14},{7,15},{8,16},{9,17... | collective-permute-start | bytes 196616 | tf_op jit(solution)/shard_map/ppermute | solution.py:328
  256.5 4.7 %collective-permute-start.5 = (bf16[256,128]{1,0:T(8,128)(2,1)S(1)}, bf16[256,128]{1,0:T(8,128)(2,1)S(1)}, u32[]{:S(2)}, u32[]{:S(2)}) collective-permute-start(bf16[256,128]{1,0:T(8,128)(2,1)S(1)} %get-tuple-element.22), channel_id=1, source_target_pairs={{0,16},{1,17},{2,18},{3,19},{4,20},{5,21},{6,22},{7,23},{8,24},{9,... | collective-permute-start | bytes 196616 | tf_op jit(solution)/shard_map/ppermute | solution.py:328
  258.8 3.1 %collective-permute-start.6 = (bf16[256,128]{1,0:T(8,128)(2,1)S(1)}, bf16[256,128]{1,0:T(8,128)(2,1)S(1)}, u32[]{:S(2)}, u32[]{:S(2)}) collective-permute-start(bf16[256,128]{1,0:T(8,128)(2,1)S(1)} %get-tuple-element.21), channel_id=1, source_target_pairs={{0,24},{1,25},{2,26},{3,27},{4,28},{5,29},{6,30},{7,31},{8,0},{9,1... | collective-permute-start | bytes 196616 | tf_op jit(solution)/shard_map/ppermute | solution.py:328

commit v4 on v3

--- a/solution.py
+++ b/solution.py
@@ -14,6 +14,7 @@
 GROUP = 4
 CHIPS_Z = 4
 CHIPS_X = 4
+INTEGRAL_VMEM = 44 * 1024 * 1024
 
 
 def tile_view(array):
@@ -22,7 +23,7 @@
     return split.transpose(0, 1, 3, 2, 4).reshape(rows * cols, comps * (pairs // LANES), LANES)
 
 
-def direct_kernel(tiles_ref, swap_ref, move_ref, move_perm_ref, weight_ref, out_ref, flat, turned, turned_perm, stage, stage_perm):
+def direct_kernel(live_ref, tiles_ref, swap_ref, move_ref, move_perm_ref, weight_ref, out_ref, flat, turned, turned_perm, stage, stage_perm):
     tiles = tiles_ref.shape[0]
     groups = tiles // GROUP
     flat[...] = tiles_ref[...].reshape(tiles * 2 * PAIRS, LANES).astype(jnp.float32)
@@ -63,23 +64,26 @@
         )
         for item in range(GROUP):
             cols = slice(item * LANES, (item + 1) * LANES)
+            live = live_ref[pl.program_id(0) * tiles + index * GROUP + item] > 0
+            kept = jnp.where(live, weight, 0.0)
             a_real = plain[:PAIRS, cols]
             a_imag = plain[PAIRS:, cols]
             b_real = moved[:PAIRS, cols]
             b_imag = moved[PAIRS:, cols]
-            out_ref[index * GROUP + item, 0] = weight * (a_real * b_real - a_imag * b_imag)
-            out_ref[index * GROUP + item, 1] = weight * (a_real * b_imag + a_imag * b_real)
+            out_ref[index * GROUP + item, 0] = kept * (a_real * b_real - a_imag * b_imag)
+            out_ref[index * GROUP + item, 1] = kept * (a_real * b_imag + a_imag * b_real)
         return carry
 
     lax.fori_loop(0, groups, one_product, 0)
 
 
-def direct_part(tiles, swap, move, move_perm, weight, block=32):
+def direct_part(live, tiles, swap, move, move_perm, weight, block=32):
     count = tiles.shape[0]
     return pl.pallas_call(
         direct_kernel,
         grid=(count // block,),
         in_specs=[
+            pl.BlockSpec(memory_space=pltpu.SMEM),
             pl.BlockSpec((block, 2 * PAIRS, LANES), lambda n: (n, 0, 0)),
             pl.BlockSpec(swap.shape, lambda n: (0, 0)),
             pl.BlockSpec(move.shape, lambda n: (0, 0)),
@@ -99,7 +103,7 @@
             flops=count * 64 * 512 * 512, bytes_accessed=count * 49152, transcendentals=0
         ),
         name="direct_part",
-    )(tiles, swap, move, move_perm, weight)
+    )(live, tiles, swap, move, move_perm, weight)
 
 
 def mirror_kernel(direct_ref, tiles_ref, out_ref, flat):
@@ -135,42 +139,13 @@
     )(direct, tiles)
 
 
-def integral_kernel(place_ref, live_ref, first_hbm, direct_hbm, tiles_hbm, slab_hbm, out_ref, first_buf, direct_buf, tiles_buf, slab_ref, flat, right, sems, slab_sem):
-    number, moments, steps = tiles_buf.shape[:3]
-    step = pl.program_id(0)
-    slab_copy = pltpu.make_async_copy(slab_hbm, slab_ref, slab_sem)
-
-    def copies(index):
-        where = (place_ref[1] + index) % CHIPS_X
-        return [
-            pltpu.make_async_copy(
-                source.at[:, where, place_ref[0]], target.at[index], sems.at[kind, index]
-            )
-            for kind, (source, target) in enumerate(
-                ((tiles_hbm, tiles_buf), (first_hbm, first_buf), (direct_hbm, direct_buf))
-            )
-        ]
-
-    @pl.when(step == 0)
-    def _():
-        for index in range(number):
-            for copy in copies(index):
-                copy.start()
-            if index == 0:
-                slab_copy.start()
-
-    for copy in copies(step):
-        copy.wait()
-    first_ref = first_buf.at[step]
-    direct_ref = direct_buf.at[step]
-    across = (place_ref[1] + pl.program_id(0)) % CHIPS_X
+def integral_kernel(place_ref, first_ref, direct_ref, tiles_ref, slab_ref, out_ref, flat, right):
+    moments, steps = tiles_ref.shape[:2]
     depth = steps * 2 * PAIRS
-    flat[...] = tiles_buf[step].reshape(moments * depth, LANES).astype(jnp.float32)
+    flat[...] = tiles_ref[...].reshape(moments * depth, LANES).astype(jnp.float32)
     low = lax.broadcasted_iota(jnp.int32, (PAIRS, LANES), 1) < ORB
 
     def retarded(moment, item):
-        time = moment * (2 * CHIPS_X) + across * 2 + place_ref[0]
-        live = live_ref[time * steps + item] > 0
         base = (moment * steps + item) * 2 * PAIRS
         m_real = flat[pl.ds(base, PAIRS, stride=2), :]
         m_imag = flat[pl.ds(base + 1, PAIRS, stride=2), :]
@@ -178,7 +153,7 @@
         d_imag = direct_ref[moment, item, 1]
         ret_real = first_ref[moment, item, 0] - (d_real * m_real - d_imag * m_imag)
         ret_imag = first_ref[moment, item, 1] - (d_real * m_imag + d_imag * m_real)
-        return jnp.where(live, ret_real, 0.0), jnp.where(live, ret_imag, 0.0)
+        return ret_real, ret_imag
 
     for pair in range(moments // 2):
         cols = slice(pair * LANES, (pair + 1) * LANES)
@@ -187,18 +162,12 @@
             other = retarded(2 * pair + 1, item)
             for comp in range(2):
                 row = (item * 2 + comp) * PAIRS
-                crossed = pltpu.roll(jnp.where(low, other[comp], left[comp]), ORB, 1)
-                right[row : row + PAIRS, cols] = jnp.where(low, left[comp], crossed).astype(
-                    jnp.bfloat16
-                )
+                right[row : row + PAIRS, cols] = jnp.where(
+                    low, left[comp], pltpu.roll(other[comp], ORB, 1)
+                ).astype(jnp.bfloat16)
                 right[depth + row : depth + row + PAIRS, cols] = jnp.where(
-                    low, crossed, other[comp]
+                    low, pltpu.roll(left[comp], ORB, 1), other[comp]
                 ).astype(jnp.bfloat16)
-
-    @pl.when(step == 0)
-    def _():
-        slab_copy.wait()
-
     product = jnp.dot(slab_ref[...], right[...], preferred_element_type=jnp.float32)
     half = product.shape[0] // 2
     lower = lax.broadcasted_iota(jnp.int32, (half, LANES), 1) < ORB
@@ -212,36 +181,43 @@
         out_ref[(slot + 1) % CHIPS_Z] = jnp.where(lower, crossed, imag)
 
 
-def integral_part(place, live, first, direct, tiles, slab, steps):
+def integral_part(place, first, direct, tiles, slab, steps):
     first = first.reshape(CHIPS_Z, CHIPS_X, 2, steps, 2, PAIRS, LANES)
     direct = direct.reshape(CHIPS_Z, CHIPS_X, 2, steps, 2, PAIRS, LANES)
     tiles = tiles.reshape(CHIPS_Z, CHIPS_X, 2, steps, 2 * PAIRS, LANES)
+    full = pl.BlockSpec(
+        (CHIPS_Z, None, None, steps, 2, PAIRS, LANES),
+        lambda n, p: (0, (p[1] + n) % CHIPS_X, p[0], 0, 0, 0, 0),
+    )
     return pl.pallas_call(
         integral_kernel,
         grid_spec=pltpu.PrefetchScalarGridSpec(
-            num_scalar_prefetch=2,
+            num_scalar_prefetch=1,
             grid=(CHIPS_X,),
-            in_specs=[pl.BlockSpec(memory_space=pl.ANY)] * 4,
+            in_specs=[
+                full,
+                full,
+                pl.BlockSpec(
+                    (CHIPS_Z, None, None, steps, 2 * PAIRS, LANES),
+                    lambda n, p: (0, (p[1] + n) % CHIPS_X, p[0], 0, 0, 0),
+                ),
+                pl.BlockSpec(slab.shape, lambda n, p: (0, 0)),
+            ],
             out_specs=pl.BlockSpec(
-                (None, CHIPS_Z, TW * ORB, LANES), lambda n, p, v: (n, 0, 0, 0)
+                (None, CHIPS_Z, TW * ORB, LANES), lambda n, p: (n, 0, 0, 0)
             ),
             scratch_shapes=[
-                pltpu.VMEM((CHIPS_X, CHIPS_Z, steps, 2, PAIRS, LANES), jnp.float32),
-                pltpu.VMEM((CHIPS_X, CHIPS_Z, steps, 2, PAIRS, LANES), jnp.float32),
-                pltpu.VMEM((CHIPS_X, CHIPS_Z, steps, 2 * PAIRS, LANES), jnp.bfloat16),
-                pltpu.VMEM(slab.shape, slab.dtype),
                 pltpu.VMEM((CHIPS_Z * steps * 2 * PAIRS, LANES), jnp.float32),
                 pltpu.VMEM((slab.shape[1], CHIPS_Z // 2 * LANES), jnp.bfloat16),
-                pltpu.SemaphoreType.DMA((3, CHIPS_X)),
-                pltpu.SemaphoreType.DMA,
             ],
         ),
         out_shape=jax.ShapeDtypeStruct((CHIPS_X, CHIPS_Z, TW * ORB, LANES), jnp.float32),
         cost_estimate=pl.CostEstimate(
             flops=16 * 1024 * 512 * 128, bytes_accessed=128 * 81920, transcendentals=0
         ),
+        compiler_params=pltpu.CompilerParams(vmem_limit_bytes=INTEGRAL_VMEM),
         name="integral_part",
-    )(place, live, first, direct, tiles, slab)
+    )(place, first, direct, tiles, slab)
 
 
 def per_device(g_greater, g_lesser, coupling, partner, memory_start):
@@ -271,10 +247,23 @@
     move_perm = (same & (src_orbit[:, None] == wanted[None, :])).astype(jnp.bfloat16)
     weight = coupling.T.reshape(PAIRS, LANES)
 
-    direct_lesser = direct_part(tiles_lesser, swap, move, move_perm, weight)
-    direct_greater = direct_part(tiles_greater, swap, move, move_perm, weight)
-    tiles_greater, direct_lesser, direct_greater = lax.optimization_barrier(
-        (tiles_greater, direct_lesser, direct_greater)
+    first_times = lax.axis_index("row") * tile_rows + jnp.arange(tile_rows, dtype=jnp.int32)
+    second_times = jnp.arange(tile_cols, dtype=jnp.int32) * col_count + lax.axis_index("col")
+    live = (second_times[None, :] >= memory_start[:, None]) & (
+        second_times[None, :] <= first_times[:, None]
+    )
+    live = live.astype(jnp.int32).reshape(tile_rows * tile_cols)
+    column = lax.axis_index("col")
+    core = column % 2
+    along = column // 2 % CHIPS_X
+    depth = column // (2 * CHIPS_X)
+    place_away = jnp.stack([1 - core, along, depth])
+    place_kept = jnp.stack([core, along, depth])
+
+    direct_lesser = direct_part(live, tiles_lesser, swap, move, move_perm, weight)
+    direct_greater = direct_part(live, tiles_greater, swap, move, move_perm, weight)
+    tiles_greater, direct_lesser, direct_greater, place_away, place_kept = lax.optimization_barrier(
+        (tiles_greater, direct_lesser, direct_greater, place_away, place_kept)
     )
     flip_greater = lax.all_to_all(tiles_greater, both, 0, 0, tiled=True)
     first = mirror_part(direct_greater, flip_lesser)
@@ -288,22 +277,12 @@
     slab = slab.transpose(0, 2, 6, 5, 3, 1, 4).reshape(
         2 * TW * orbits, 2 * tile_cols * 2 * PAIRS
     )
-    first_times = lax.axis_index("row") * tile_rows + jnp.arange(tile_rows, dtype=jnp.int32)
-    second_times = jnp.arange(tile_cols, dtype=jnp.int32) * col_count + lax.axis_index("col")
-    live = (second_times[None, :] >= memory_start[:, None]) & (
-        second_times[None, :] <= first_times[:, None]
-    )
-    live = live.astype(jnp.int32).reshape(tile_rows * tile_cols)
-    column = lax.axis_index("col")
-    core = column % 2
-    along = column // 2 % CHIPS_X
-    depth = column // (2 * CHIPS_X)
     away = integral_part(
-        jnp.stack([1 - core, along, depth]), live, first, direct_lesser, flip_greater, slab, tile_cols
+        place_away, first, direct_lesser, flip_greater, slab, tile_cols
     )
     arrived = lax.ppermute(away, "col", [(item, item ^ 1) for item in range(col_count)])
     kept = integral_part(
-        jnp.stack([core, along, depth]), live, first, direct_lesser, flip_greater, slab, tile_cols
+        place_kept, first, direct_lesser, flip_greater, slab, tile_cols
     )
     places = [
         (z, x, side) for z in range(CHIPS_Z) for x in range(CHIPS_X) for side in range(2)

time: 266 us -> 260 us (0.977)
  Pallas kernels: 115 us -> 111 us
  other arithmetic: 6.75 us -> 3.21 us
    pallas_call x2, Pallas kernels: 18.2 us -> 13.7 us  [integral_part(): pl.pallas_call(integral_kernel, grid_spec=pltpu.PrefetchScalarGridSpec(nu...]
  transfers between devices with their start and end apart: 9 -> 9, of which waited for: 8 -> 8; matrix products, arithmetic and copies ran while one was open for 5% -> 4% of each run, Pallas kernels for 40% -> 41%
where the time goes in v4:
time: 260 us; the launch traced here: 257 us
  Pallas kernels  111 us (43%)
  waiting for transfers between devices  97.5 us (38%)
  starting transfers between devices  35.1 us (14%)
  local copies, waits for them, and re-layouts  9.64 us (4%)
  other arithmetic  3.21 us (1%)
    pallas_call x2, Pallas kernels, direct_part(): pl.pallas_call(direct_kernel, grid=(count // block,), in_specs=[pl.BlockS...  86.9 us
    all_to_all x1, waiting for transfers between devices, per_device(): flip_greater = lax.all_to_all(tiles_greater, both, 0, 0, tiled=True)  78.5 us
    all_to_all x1, starting transfers between devices, per_device(): flip_lesser = lax.all_to_all(tiles_lesser, both, 0, 0, tiled=True)  16.7 us
    pallas_call x2, Pallas kernels, integral_part(): pl.pallas_call(integral_kernel, grid_spec=pltpu.PrefetchScalarGridSpec(nu...  13.7 us
    ppermute x3, waiting for transfers between devices, per_device(): lax.ppermute((kept[shift] + arrived[shift]).astype(jnp.bfloat16), 'col',...  12.3 us
    pallas_call x1, Pallas kernels, mirror_part(): pl.pallas_call(mirror_kernel, grid=(count // block,), in_specs=[full, pl....  10.4 us
    all_to_all x1, starting transfers between devices, per_device(): flip_greater = lax.all_to_all(tiles_greater, both, 0, 0, tiled=True)  9.57 us
  transfers between devices with their start and end apart: 9, of which 8 were waited for; matrix products, arithmetic and copies ran while one was open for 4% of the time, Pallas kernels for 41%

profile of v4, /device:TPU:1, one launch (start us, length us, event | category | flops | bytes accessed | tf_op | source)
XLA Modules:
  0.0 256.7 jit_solution(8343797963591624792)
XLA Ops:
  0.0 16.7 %all-to-all-start = ((bf16[256,64,128]{2,1,0:T(8,128)(2,1)}), bf16[256,64,128]{2,1,0:T(8,128)(2,1)}, u32[]{:S(2)}, u32[]{:S(2)}) async-start(bf16[256,64,128]{2,1,0:T(8,128)(2,1)} %bitcast.72), calls=%async_computation | async-start | bytes 8388608 | tf_op jit(solution)/shard_map/all_to_all | solution.py:231
  17.0 0.7 reshape.247.live_ref
  17.8 0.7 mul.57.swap_ref
  18.6 0.7 reshape.241.weight_ref
  19.3 1.5 and_convert_fusion
  20.8 43.5 %direct_part.2 = f32[256,2,32,128]{3,2,1,0:T(8,128)} custom-call(s32[256]{0:T(256)} %reshape.247.live_ref, bf16[256,64,128]{2,1,0:T(8,128)(2,1)} %bitcast.73, bf16[128,128]{1,0:T(8,128)(2,1)} %mul.57.swap_ref, bf16[512,512]{1,0:T(8,128)(2,1)} %get-tuple-element.28.move_ref, bf16[512,512]{1,0:T(8,128)(2,1)} %get-tuple-element.27.move_perm_ref, ...), custom_call_target="tpu_custom_call" | custom-call | flops 4294967296 | bytes 12582912 | tf_op jit(solution)/shard_map/direct_part/pallas_call | solution.py:82
  64.4 43.4 %direct_part.3.direct_ref = f32[256,2,32,128]{3,2,1,0:T(8,128)} custom-call(s32[256]{0:T(256)} %reshape.247.live_ref, bf16[256,64,128]{2,1,0:T(8,128)(2,1)} %bitcast.74, bf16[128,128]{1,0:T(8,128)(2,1)} %mul.57.swap_ref, bf16[512,512]{1,0:T(8,128)(2,1)} %get-tuple-element.28.move_ref, bf16[512,512]{1,0:T(8,128)(2,1)} %get-tuple-element.27.move_perm_ref, ...), custom_call_target="tpu_custom_call" | custom-call | flops 4294967296 | bytes 12582912 | tf_op jit(solution)/shard_map/direct_part/pallas_call | solution.py:82
  107.8 5.1 %all-to-all-done.tiles_ref = bf16[256,64,128]{2,1,0:T(8,128)(2,1)} async-done(((bf16[256,64,128]{2,1,0:T(8,128)(2,1)}), bf16[256,64,128]{2,1,0:T(8,128)(2,1)}, u32[]{:S(2)}, u32[]{:S(2)}) %all-to-all-start) | async-done | bytes 4194336 | tf_op jit(solution)/shard_map/all_to_all | solution.py:231
  112.9 9.6 %all-to-all-start.1 = ((bf16[256,64,128]{2,1,0:T(8,128)(2,1)}), bf16[256,64,128]{2,1,0:T(8,128)(2,1)}, u32[]{:S(2)}, u32[]{:S(2)}) async-start(bf16[256,64,128]{2,1,0:T(8,128)(2,1)} %bitcast.75), calls=%async_computation.1 | async-start | bytes 8388608 | tf_op jit(solution)/shard_map/all_to_all | solution.py:268
  122.5 1.1 slice.63
  123.6 0.4 reshape.245
  124.0 1.1 fusion.40
  125.5 0.5 maximum_bitcast_fusion.1
  126.0 0.5 maximum_bitcast_fusion
  126.5 1.6 copy.27
  128.1 1.3 reshape.246
  129.4 0.5 copy.28.slab_ref
  129.9 10.4 %mirror_part.1 = f32[256,2,32,128]{3,2,1,0:T(8,128)} custom-call(f32[256,2,32,128]{3,2,1,0:T(8,128)} %direct_part.3.direct_ref, bf16[256,64,128]{2,1,0:T(8,128)(2,1)} %all-to-all-done.tiles_ref), custom_call_target="tpu_custom_call" | custom-call | flops 16777216 | bytes 20971520 | tf_op jit(solution)/shard_map/mirror_part/pallas_call | solution.py:128
  140.3 78.5 %all-to-all-done.1 = bf16[256,64,128]{2,1,0:T(8,128)(2,1)} async-done(((bf16[256,64,128]{2,1,0:T(8,128)(2,1)}), bf16[256,64,128]{2,1,0:T(8,128)(2,1)}, u32[]{:S(2)}, u32[]{:S(2)}) %all-to-all-start.1) | async-done | bytes 4194336 | tf_op jit(solution)/shard_map/all_to_all | solution.py:268
  218.8 6.9 %integral_part.3 = f32[4,4,256,128]{3,2,1,0:T(8,128)S(1)} custom-call(s32[3]{0:T(128)S(1)} %get-tuple-element.14.place_ref, f32[4,4,2,8,2,32,128]{6,5,4,3,2,1,0:T(8,128)} %bitcast.68, f32[4,4,2,8,2,32,128]{6,5,4,3,2,1,0:T(8,128)} %bitcast.70, bf16[4,4,2,8,64,128]{5,4,3,2,1,0:T(8,128)(2,1)} %bitcast.17.tiles_ref, bf16[512,1024]{1,0:T(8,128)(2,1)S(1)} %copy.28.slab_ref), custom_call_target="tpu_custom_call" | custom-call | flops 1073741824 | bytes 10485760 | tf_op jit(solution)/shard_map/integral_part/pallas_call | solution.py:192
  225.7 1.6 collective-permute-start
  227.3 6.9 %integral_part.2 = f32[4,4,256,128]{3,2,1,0:T(8,128)S(1)} custom-call(s32[3]{0:T(128)S(1)} %get-tuple-element.10.place_ref, f32[4,4,2,8,2,32,128]{6,5,4,3,2,1,0:T(8,128)} %bitcast.69, f32[4,4,2,8,2,32,128]{6,5,4,3,2,1,0:T(8,128)} %bitcast.71, bf16[4,4,2,8,64,128]{5,4,3,2,1,0:T(8,128)(2,1)} %bitcast.17.tiles_ref, bf16[512,1024]{1,0:T(8,128)(2,1)S(1)} %copy.28.slab_ref), custom_call_target="tpu_custom_call" | custom-call | flops 1073741824 | bytes 10485760 | tf_op jit(solution)/shard_map/integral_part/pallas_call | solution.py:192
  234.6 2.5 collective-permute-start.2
  237.3 7.0 %collective-permute-done.1 = bf16[4,256,128]{2,1,0:T(8,128)(2,1)S(1)} collective-permute-done((bf16[4,256,128]{2,1,0:T(8,128)(2,1)S(1)}, bf16[4,256,128]{2,1,0:T(8,128)(2,1)S(1)}, u32[]{:S(2)}, u32[]{:S(2)}) %collective-permute-start.1) | collective-permute-done | bytes 262176 | tf_op jit(solution)/shard_map/ppermute | solution.py:296
  244.3 4.3 %collective-permute-done.2 = bf16[4,256,128]{2,1,0:T(8,128)(2,1)S(1)} collective-permute-done((bf16[4,256,128]{2,1,0:T(8,128)(2,1)S(1)}, bf16[4,256,128]{2,1,0:T(8,128)(2,1)S(1)}, u32[]{:S(2)}, u32[]{:S(2)}) %collective-permute-start.2) | collective-permute-done | bytes 262176 | tf_op jit(solution)/shard_map/ppermute | solution.py:296
  248.6 1.0 collective-permute-done.3
  249.8 0.5 collective-permute-start.4
  250.2 2.3 collective-permute-start.5
  252.5 1.5 collective-permute-start.6
  254.0 0.8 collective-permute-done.4
  255.0 0.7 collective-permute-done.6
  255.9 0.8 convert_element_type.122
  (32 shorter events, 2.1 us)
Async XLA Ops:
  0.0 16.7 %copy-start.1 = (s32[64]{0:T(128)S(1)}, s32[64]{0:T(128)}, u32[]{:S(2)}) copy-start(s32[64]{0:T(128)} %param.8) | copy-start | bytes 772
  0.0 16.8 %copy-start.2 = (s32[32]{0:T(128)S(1)}, s32[32]{0:T(128)}, u32[]{:S(2)}) copy-start(s32[32]{0:T(128)} %param.9) | copy-start | bytes 388
  0.0 18.5 %copy-start = (f32[64,64]{1,0:T(8,128)S(1)}, f32[64,64]{1,0:T(8,128)}, u32[]{:S(2)}) copy-start(f32[64,64]{1,0:T(8,128)} %param.7) | copy-start | bytes 49156
  0.0 112.9 %all-to-all-start = ((bf16[256,64,128]{2,1,0:T(8,128)(2,1)}), bf16[256,64,128]{2,1,0:T(8,128)(2,1)}, u32[]{:S(2)}, u32[]{:S(2)}) async-start(bf16[256,64,128]{2,1,0:T(8,128)(2,1)} %bitcast.72), calls=%async_computation | async-start | bytes 8388608 | tf_op jit(solution)/shard_map/all_to_all | solution.py:231
  112.9 105.8 %all-to-all-start.1 = ((bf16[256,64,128]{2,1,0:T(8,128)(2,1)}), bf16[256,64,128]{2,1,0:T(8,128)(2,1)}, u32[]{:S(2)}, u32[]{:S(2)}) async-start(bf16[256,64,128]{2,1,0:T(8,128)(2,1)} %bitcast.75), calls=%async_computation.1 | async-start | bytes 8388608 | tf_op jit(solution)/shard_map/all_to_all | solution.py:268
  225.7 8.5 %collective-permute-start = (f32[4,4,256,128]{3,2,1,0:T(8,128)S(1)}, f32[4,4,256,128]{3,2,1,0:T(8,128)S(1)}, u32[]{:S(2)}, u32[]{:S(2)}) collective-permute-start(f32[4,4,256,128]{3,2,1,0:T(8,128)S(1)} %integral_part.3), channel_id=1, source_target_pairs={{0,1},{1,0},{2,3},{3,2},{4,5},{5,4},{6,7},{7,6},{8,9},{9,8},{10,11... | collective-permute-start | bytes 6291464 | tf_op jit(solution)/shard_map/ppermute | solution.py:283
  234.3 10.0 %collective-permute-start.1 = (bf16[4,256,128]{2,1,0:T(8,128)(2,1)S(1)}, bf16[4,256,128]{2,1,0:T(8,128)(2,1)S(1)}, u32[]{:S(2)}, u32[]{:S(2)}) collective-permute-start(bf16[4,256,128]{2,1,0:T(8,128)(2,1)S(1)} %get-tuple-element.17), channel_id=1, source_target_pairs={{0,2},{1,3},{2,4},{3,5},{4,6},{5,7},{6,0},{7,1},{8,10},{9,11},{10,... | collective-permute-start | bytes 786440 | tf_op jit(solution)/shard_map/ppermute | solution.py:296
  234.6 14.0 %collective-permute-start.2 = (bf16[4,256,128]{2,1,0:T(8,128)(2,1)S(1)}, bf16[4,256,128]{2,1,0:T(8,128)(2,1)S(1)}, u32[]{:S(2)}, u32[]{:S(2)}) collective-permute-start(bf16[4,256,128]{2,1,0:T(8,128)(2,1)S(1)} %get-tuple-element.19), channel_id=1, source_target_pairs={{0,4},{1,5},{2,6},{3,7},{4,0},{5,1},{6,2},{7,3},{8,12},{9,13},{10,... | collective-permute-start | bytes 786440 | tf_op jit(solution)/shard_map/ppermute | solution.py:296
  237.1 12.5 %collective-permute-start.3 = (bf16[4,256,128]{2,1,0:T(8,128)(2,1)S(1)}, bf16[4,256,128]{2,1,0:T(8,128)(2,1)S(1)}, u32[]{:S(2)}, u32[]{:S(2)}) collective-permute-start(bf16[4,256,128]{2,1,0:T(8,128)(2,1)S(1)} %get-tuple-element.18), channel_id=1, source_target_pairs={{0,6},{1,7},{2,0},{3,1},{4,2},{5,3},{6,4},{7,5},{8,14},{9,15},{10,... | collective-permute-start | bytes 786440 | tf_op jit(solution)/shard_map/ppermute | solution.py:296
  249.8 5.1 %collective-permute-start.4 = (bf16[256,128]{1,0:T(8,128)(2,1)S(1)}, bf16[256,128]{1,0:T(8,128)(2,1)S(1)}, u32[]{:S(2)}, u32[]{:S(2)}) collective-permute-start(bf16[256,128]{1,0:T(8,128)(2,1)S(1)} %get-tuple-element.24), channel_id=1, source_target_pairs={{0,8},{1,9},{2,10},{3,11},{4,12},{5,13},{6,14},{7,15},{8,16},{9,17... | collective-permute-start | bytes 196616 | tf_op jit(solution)/shard_map/ppermute | solution.py:307
  250.2 4.7 %collective-permute-start.5 = (bf16[256,128]{1,0:T(8,128)(2,1)S(1)}, bf16[256,128]{1,0:T(8,128)(2,1)S(1)}, u32[]{:S(2)}, u32[]{:S(2)}) collective-permute-start(bf16[256,128]{1,0:T(8,128)(2,1)S(1)} %get-tuple-element.26), channel_id=1, source_target_pairs={{0,16},{1,17},{2,18},{3,19},{4,20},{5,21},{6,22},{7,23},{8,24},{9,... | collective-permute-start | bytes 196616 | tf_op jit(solution)/shard_map/ppermute | solution.py:307
  252.5 3.1 %collective-permute-start.6 = (bf16[256,128]{1,0:T(8,128)(2,1)S(1)}, bf16[256,128]{1,0:T(8,128)(2,1)S(1)}, u32[]{:S(2)}, u32[]{:S(2)}) collective-permute-start(bf16[256,128]{1,0:T(8,128)(2,1)S(1)} %get-tuple-element.25), channel_id=1, source_target_pairs={{0,24},{1,25},{2,26},{3,27},{4,28},{5,29},{6,30},{7,31},{8,0},{9,1... | collective-permute-start | bytes 196616 | tf_op jit(solution)/shard_map/ppermute | solution.py:307

commit v5 on v4

--- a/solution.py
+++ b/solution.py
@@ -14,7 +14,7 @@
 GROUP = 4
 CHIPS_Z = 4
 CHIPS_X = 4
-INTEGRAL_VMEM = 44 * 1024 * 1024
+INTEGRAL_VMEM = 48 * 1024 * 1024
 
 
 def tile_view(array):
@@ -298,7 +298,7 @@
             "col",
             [(name_of(z, x, side), name_of(z, x + shift, side)) for z, x, side in places],
         )
-        for shift in range(1, CHIPS_X)
+        for shift in (2, 1, 3)
     ]
     for part in parts:
         summed = summed + part.astype(jnp.float32)

time: 260 us -> 259 us (level); the launches traced: 257 us -> 259 us
  transfers between devices with their start and end apart: 9 -> 9, of which waited for: 8 -> 6; matrix products, arithmetic and copies ran while one was open for 4% -> 4% of each run, Pallas kernels for 41% -> 40%
where the time goes in v5:
time: 259 us
  Pallas kernels  111 us (43%)
  waiting for transfers between devices  99 us (38%)
  starting transfers between devices  35.7 us (14%)
  local copies, waits for them, and re-layouts  9.64 us (4%)
  other arithmetic  3.21 us (1%)
    pallas_call x2, Pallas kernels, direct_part(): pl.pallas_call(direct_kernel, grid=(count // block,), in_specs=[pl.BlockS...  86.9 us
    all_to_all x1, waiting for transfers between devices, per_device(): flip_greater = lax.all_to_all(tiles_greater, both, 0, 0, tiled=True)  78.5 us
    all_to_all x1, starting transfers between devices, per_device(): flip_lesser = lax.all_to_all(tiles_lesser, both, 0, 0, tiled=True)  16.7 us
    pallas_call x2, Pallas kernels, integral_part(): pl.pallas_call(integral_kernel, grid_spec=pltpu.PrefetchScalarGridSpec(nu...  13.7 us
    ppermute x3, waiting for transfers between devices, per_device(): lax.ppermute((kept[shift] + arrived[shift]).astype(jnp.bfloat16), 'col',...  12 us
    pallas_call x1, Pallas kernels, mirror_part(): pl.pallas_call(mirror_kernel, grid=(count // block,), in_specs=[full, pl....  10.4 us
    all_to_all x1, starting transfers between devices, per_device(): flip_greater = lax.all_to_all(tiles_greater, both, 0, 0, tiled=True)  9.57 us
  transfers between devices with their start and end apart: 9, of which 6 were waited for; matrix products, arithmetic and copies ran while one was open for 4% of the time, Pallas kernels for 40%

profile of v5, /device:TPU:1, one launch (start us, length us, event | category | flops | bytes accessed | tf_op | source)
XLA Modules:
  0.0 258.9 jit_solution(4724884227774723544)
XLA Ops:
  0.0 16.7 %all-to-all-start = ((bf16[256,64,128]{2,1,0:T(8,128)(2,1)}), bf16[256,64,128]{2,1,0:T(8,128)(2,1)}, u32[]{:S(2)}, u32[]{:S(2)}) async-start(bf16[256,64,128]{2,1,0:T(8,128)(2,1)} %bitcast.72), calls=%async_computation | async-start | bytes 8388608 | tf_op jit(solution)/shard_map/all_to_all | solution.py:231
  17.0 0.7 reshape.247.live_ref
  17.8 0.7 mul.57.swap_ref
  18.6 0.7 reshape.241.weight_ref
  19.3 1.5 and_convert_fusion
  20.8 43.5 %direct_part.2 = f32[256,2,32,128]{3,2,1,0:T(8,128)} custom-call(s32[256]{0:T(256)} %reshape.247.live_ref, bf16[256,64,128]{2,1,0:T(8,128)(2,1)} %bitcast.73, bf16[128,128]{1,0:T(8,128)(2,1)} %mul.57.swap_ref, bf16[512,512]{1,0:T(8,128)(2,1)} %get-tuple-element.28.move_ref, bf16[512,512]{1,0:T(8,128)(2,1)} %get-tuple-element.27.move_perm_ref, ...), custom_call_target="tpu_custom_call" | custom-call | flops 4294967296 | bytes 12582912 | tf_op jit(solution)/shard_map/direct_part/pallas_call | solution.py:82
  64.4 43.4 %direct_part.3.direct_ref = f32[256,2,32,128]{3,2,1,0:T(8,128)} custom-call(s32[256]{0:T(256)} %reshape.247.live_ref, bf16[256,64,128]{2,1,0:T(8,128)(2,1)} %bitcast.74, bf16[128,128]{1,0:T(8,128)(2,1)} %mul.57.swap_ref, bf16[512,512]{1,0:T(8,128)(2,1)} %get-tuple-element.28.move_ref, bf16[512,512]{1,0:T(8,128)(2,1)} %get-tuple-element.27.move_perm_ref, ...), custom_call_target="tpu_custom_call" | custom-call | flops 4294967296 | bytes 12582912 | tf_op jit(solution)/shard_map/direct_part/pallas_call | solution.py:82
  107.8 5.1 %all-to-all-done.tiles_ref = bf16[256,64,128]{2,1,0:T(8,128)(2,1)} async-done(((bf16[256,64,128]{2,1,0:T(8,128)(2,1)}), bf16[256,64,128]{2,1,0:T(8,128)(2,1)}, u32[]{:S(2)}, u32[]{:S(2)}) %all-to-all-start) | async-done | bytes 4194336 | tf_op jit(solution)/shard_map/all_to_all | solution.py:231
  112.9 9.6 %all-to-all-start.1 = ((bf16[256,64,128]{2,1,0:T(8,128)(2,1)}), bf16[256,64,128]{2,1,0:T(8,128)(2,1)}, u32[]{:S(2)}, u32[]{:S(2)}) async-start(bf16[256,64,128]{2,1,0:T(8,128)(2,1)} %bitcast.75), calls=%async_computation.1 | async-start | bytes 8388608 | tf_op jit(solution)/shard_map/all_to_all | solution.py:268
  122.5 1.1 slice.63
  124.0 1.1 fusion.40
  125.5 0.5 maximum_bitcast_fusion.1
  126.0 0.5 maximum_bitcast_fusion
  126.5 1.6 copy.27
  128.1 1.3 reshape.246
  129.4 0.5 copy.28.slab_ref
  129.9 10.4 %mirror_part.1 = f32[256,2,32,128]{3,2,1,0:T(8,128)} custom-call(f32[256,2,32,128]{3,2,1,0:T(8,128)} %direct_part.3.direct_ref, bf16[256,64,128]{2,1,0:T(8,128)(2,1)} %all-to-all-done.tiles_ref), custom_call_target="tpu_custom_call" | custom-call | flops 16777216 | bytes 20971520 | tf_op jit(solution)/shard_map/mirror_part/pallas_call | solution.py:128
  140.3 78.5 %all-to-all-done.1 = bf16[256,64,128]{2,1,0:T(8,128)(2,1)} async-done(((bf16[256,64,128]{2,1,0:T(8,128)(2,1)}), bf16[256,64,128]{2,1,0:T(8,128)(2,1)}, u32[]{:S(2)}, u32[]{:S(2)}) %all-to-all-start.1) | async-done | bytes 4194336 | tf_op jit(solution)/shard_map/all_to_all | solution.py:268
  218.8 6.9 %integral_part.3 = f32[4,4,256,128]{3,2,1,0:T(8,128)S(1)} custom-call(s32[3]{0:T(128)S(1)} %get-tuple-element.14.place_ref, f32[4,4,2,8,2,32,128]{6,5,4,3,2,1,0:T(8,128)} %bitcast.68, f32[4,4,2,8,2,32,128]{6,5,4,3,2,1,0:T(8,128)} %bitcast.70, bf16[4,4,2,8,64,128]{5,4,3,2,1,0:T(8,128)(2,1)} %bitcast.17.tiles_ref, bf16[512,1024]{1,0:T(8,128)(2,1)S(1)} %copy.28.slab_ref), custom_call_target="tpu_custom_call" | custom-call | flops 1073741824 | bytes 10485760 | tf_op jit(solution)/shard_map/integral_part/pallas_call | solution.py:192
  225.7 1.6 collective-permute-start
  227.3 6.9 %integral_part.2 = f32[4,4,256,128]{3,2,1,0:T(8,128)S(1)} custom-call(s32[3]{0:T(128)S(1)} %get-tuple-element.10.place_ref, f32[4,4,2,8,2,32,128]{6,5,4,3,2,1,0:T(8,128)} %bitcast.69, f32[4,4,2,8,2,32,128]{6,5,4,3,2,1,0:T(8,128)} %bitcast.71, bf16[4,4,2,8,64,128]{5,4,3,2,1,0:T(8,128)(2,1)} %bitcast.17.tiles_ref, bf16[512,1024]{1,0:T(8,128)(2,1)S(1)} %copy.28.slab_ref), custom_call_target="tpu_custom_call" | custom-call | flops 1073741824 | bytes 10485760 | tf_op jit(solution)/shard_map/integral_part/pallas_call | solution.py:192
  234.3 0.9 collective-permute-start.1
  235.2 1.2 collective-permute-start.2
  236.5 1.4 collective-permute-start.3
  237.9 6.1 %collective-permute-done.1 = bf16[4,256,128]{2,1,0:T(8,128)(2,1)S(1)} collective-permute-done((bf16[4,256,128]{2,1,0:T(8,128)(2,1)S(1)}, bf16[4,256,128]{2,1,0:T(8,128)(2,1)S(1)}, u32[]{:S(2)}, u32[]{:S(2)}) %collective-permute-start.1) | collective-permute-done | bytes 262176 | tf_op jit(solution)/shard_map/ppermute | solution.py:296
  244.0 6.0 %collective-permute-done.2 = bf16[4,256,128]{2,1,0:T(8,128)(2,1)S(1)} collective-permute-done((bf16[4,256,128]{2,1,0:T(8,128)(2,1)S(1)}, bf16[4,256,128]{2,1,0:T(8,128)(2,1)S(1)}, u32[]{:S(2)}, u32[]{:S(2)}) %collective-permute-start.2) | collective-permute-done | bytes 262176 | tf_op jit(solution)/shard_map/ppermute | solution.py:296
  250.1 0.7 collective-permute-start.4
  250.8 2.1 collective-permute-start.5
  252.9 1.5 collective-permute-start.6
  254.4 0.8 collective-permute-done.4
  255.2 2.6 collective-permute-done.5
  258.1 0.8 convert_element_type.122
  (32 shorter events, 1.9 us)
Async XLA Ops:
  0.0 16.7 %copy-start.1 = (s32[64]{0:T(128)S(1)}, s32[64]{0:T(128)}, u32[]{:S(2)}) copy-start(s32[64]{0:T(128)} %param.8) | copy-start | bytes 772
  0.0 16.8 %copy-start.2 = (s32[32]{0:T(128)S(1)}, s32[32]{0:T(128)}, u32[]{:S(2)}) copy-start(s32[32]{0:T(128)} %param.9) | copy-start | bytes 388
  0.0 18.5 %copy-start = (f32[64,64]{1,0:T(8,128)S(1)}, f32[64,64]{1,0:T(8,128)}, u32[]{:S(2)}) copy-start(f32[64,64]{1,0:T(8,128)} %param.7) | copy-start | bytes 49156
  0.0 112.9 %all-to-all-start = ((bf16[256,64,128]{2,1,0:T(8,128)(2,1)}), bf16[256,64,128]{2,1,0:T(8,128)(2,1)}, u32[]{:S(2)}, u32[]{:S(2)}) async-start(bf16[256,64,128]{2,1,0:T(8,128)(2,1)} %bitcast.72), calls=%async_computation | async-start | bytes 8388608 | tf_op jit(solution)/shard_map/all_to_all | solution.py:231
  112.9 105.8 %all-to-all-start.1 = ((bf16[256,64,128]{2,1,0:T(8,128)(2,1)}), bf16[256,64,128]{2,1,0:T(8,128)(2,1)}, u32[]{:S(2)}, u32[]{:S(2)}) async-start(bf16[256,64,128]{2,1,0:T(8,128)(2,1)} %bitcast.75), calls=%async_computation.1 | async-start | bytes 8388608 | tf_op jit(solution)/shard_map/all_to_all | solution.py:268
  225.7 8.5 %collective-permute-start = (f32[4,4,256,128]{3,2,1,0:T(8,128)S(1)}, f32[4,4,256,128]{3,2,1,0:T(8,128)S(1)}, u32[]{:S(2)}, u32[]{:S(2)}) collective-permute-start(f32[4,4,256,128]{3,2,1,0:T(8,128)S(1)} %integral_part.3), channel_id=1, source_target_pairs={{0,1},{1,0},{2,3},{3,2},{4,5},{5,4},{6,7},{7,6},{8,9},{9,8},{10,11... | collective-permute-start | bytes 6291464 | tf_op jit(solution)/shard_map/ppermute | solution.py:283
  234.3 9.7 %collective-permute-start.1 = (bf16[4,256,128]{2,1,0:T(8,128)(2,1)S(1)}, bf16[4,256,128]{2,1,0:T(8,128)(2,1)S(1)}, u32[]{:S(2)}, u32[]{:S(2)}) collective-permute-start(bf16[4,256,128]{2,1,0:T(8,128)(2,1)S(1)} %get-tuple-element.17), channel_id=1, source_target_pairs={{0,4},{1,5},{2,6},{3,7},{4,0},{5,1},{6,2},{7,3},{8,12},{9,13},{10,... | collective-permute-start | bytes 786440 | tf_op jit(solution)/shard_map/ppermute | solution.py:296
  235.2 14.7 %collective-permute-start.2 = (bf16[4,256,128]{2,1,0:T(8,128)(2,1)S(1)}, bf16[4,256,128]{2,1,0:T(8,128)(2,1)S(1)}, u32[]{:S(2)}, u32[]{:S(2)}) collective-permute-start(bf16[4,256,128]{2,1,0:T(8,128)(2,1)S(1)} %get-tuple-element.19), channel_id=1, source_target_pairs={{0,2},{1,3},{2,4},{3,5},{4,6},{5,7},{6,0},{7,1},{8,10},{9,11},{10,... | collective-permute-start | bytes 786440 | tf_op jit(solution)/shard_map/ppermute | solution.py:296
  236.5 13.5 %collective-permute-start.3 = (bf16[4,256,128]{2,1,0:T(8,128)(2,1)S(1)}, bf16[4,256,128]{2,1,0:T(8,128)(2,1)S(1)}, u32[]{:S(2)}, u32[]{:S(2)}) collective-permute-start(bf16[4,256,128]{2,1,0:T(8,128)(2,1)S(1)} %get-tuple-element.18), channel_id=1, source_target_pairs={{0,6},{1,7},{2,0},{3,1},{4,2},{5,3},{6,4},{7,5},{8,14},{9,15},{10,... | collective-permute-start | bytes 786440 | tf_op jit(solution)/shard_map/ppermute | solution.py:296
  250.1 5.1 %collective-permute-start.4 = (bf16[256,128]{1,0:T(8,128)(2,1)S(1)}, bf16[256,128]{1,0:T(8,128)(2,1)S(1)}, u32[]{:S(2)}, u32[]{:S(2)}) collective-permute-start(bf16[256,128]{1,0:T(8,128)(2,1)S(1)} %get-tuple-element.24), channel_id=1, source_target_pairs={{0,8},{1,9},{2,10},{3,11},{4,12},{5,13},{6,14},{7,15},{8,16},{9,17... | collective-permute-start | bytes 196616 | tf_op jit(solution)/shard_map/ppermute | solution.py:307
  250.8 7.0 %collective-permute-start.5 = (bf16[256,128]{1,0:T(8,128)(2,1)S(1)}, bf16[256,128]{1,0:T(8,128)(2,1)S(1)}, u32[]{:S(2)}, u32[]{:S(2)}) collective-permute-start(bf16[256,128]{1,0:T(8,128)(2,1)S(1)} %get-tuple-element.26), channel_id=1, source_target_pairs={{0,16},{1,17},{2,18},{3,19},{4,20},{5,21},{6,22},{7,23},{8,24},{9,... | collective-permute-start | bytes 196616 | tf_op jit(solution)/shard_map/ppermute | solution.py:307
  252.9 4.9 %collective-permute-start.6 = (bf16[256,128]{1,0:T(8,128)(2,1)S(1)}, bf16[256,128]{1,0:T(8,128)(2,1)S(1)}, u32[]{:S(2)}, u32[]{:S(2)}) collective-permute-start(bf16[256,128]{1,0:T(8,128)(2,1)S(1)} %get-tuple-element.25), channel_id=1, source_target_pairs={{0,24},{1,25},{2,26},{3,27},{4,28},{5,29},{6,30},{7,31},{8,0},{9,1... | collective-permute-start | bytes 196616 | tf_op jit(solution)/shard_map/ppermute | solution.py:307
